TPU v7x, 8 devices: a whole 2x2x1 slice. The times are simulated.
8 devices in a mesh: ep: 4 (over z, y, x), dp: 2 (over core).
Axes of the slice: x: 2, y: 2, z: 1, core: 2. Of those that a mesh axis runs over, the one named last changes fastest.
Arguments:
- act_in: bfloat16 [6144, 448], P(('ep', 'dp'))
- grad_out: bfloat16 [6144, 448], P(('ep', 'dp'))
- slot_ids: int32 [2, 6144, 8], P(None, ('ep', 'dp'))
- gate_vals: float32 [2, 6144, 8], P(None, ('ep', 'dp'))
- w_dense: bfloat16 [2, 448, 448], replicated
- w_gate: bfloat16 [2, 384, 448, 128], P(None, 'ep')
- w_up: bfloat16 [2, 384, 448, 128], P(None, 'ep')
- w_down: bfloat16 [2, 384, 128, 448], P(None, 'ep')
- ws_gate: bfloat16 [2, 448, 128], replicated
- ws_up: bfloat16 [2, 448, 128], replicated
- ws_down: bfloat16 [2, 128, 448], replicated
Outputs:
- output 1: bfloat16 [6144, 448], P(('ep', 'dp'))
- output 2: bfloat16 [2, 448, 448], replicated
- output 3: bfloat16 [2, 384, 448, 128], P(None, 'ep')
- output 4: bfloat16 [2, 384, 448, 128], P(None, 'ep')
- output 5: bfloat16 [2, 384, 128, 448], P(None, 'ep')
- output 6: bfloat16 [2, 448, 128], replicated
- output 7: bfloat16 [2, 448, 128], replicated
- output 8: bfloat16 [2, 128, 448], replicated
All inputs are finite; a program needn't handle non-finite values.
Results may differ from a plain program's by a relative error of at most 0.02.
Values are sent between devices in bfloat16 or wider.
A program may use at most 1 GiB of HBM per device.

v0:
```python
import functools
import jax
import jax.numpy as jnp
from jax import lax
from jax.experimental import pallas as pl
from jax.experimental.pallas import tpu as pltpu
from jax.sharding import PartitionSpec as P

ALL_AXES = ("ep", "dp")
GROUP = 8
UNROLL = 8
VMEM_LIMIT = 62 * 1024 * 1024
F32 = jnp.float32
BF16 = jnp.bfloat16


def dot(left, right, left_dim, right_dim):
    return lax.dot_general(left, right, (((left_dim,), (right_dim,)), ((), ())), preferred_element_type=F32)


def silu_parts(pre_act):
    sigma = jax.nn.sigmoid(pre_act)
    return pre_act * sigma, sigma * (1.0 + pre_act * (1.0 - sigma))


def route(meta_ref, src, first_expert, capacity, pick_ref, slot, tok_ref):
    top = meta_ref.shape[1] // 2
    tokens = meta_ref.shape[2]
    width = tok_ref.shape[1] - 4 * GROUP
    slots = meta_ref[src, 0:top, :].astype(jnp.int32)
    gates = meta_ref[src, top : 2 * top, :]
    expert = slots // capacity - first_expert
    row = (slots % capacity).astype(F32)
    which = lax.broadcasted_iota(jnp.int32, (GROUP, tokens), 0)
    row_of = jnp.full((GROUP, tokens), -1.0, F32)
    gate_of = jnp.zeros((GROUP, tokens), F32)
    for j in range(top):
        hit = expert[j : j + 1, :] == which
        row_of = jnp.where(hit, row[j : j + 1, :], row_of)
        gate_of = jnp.where(hit, gates[j : j + 1, :], gate_of)
    high = gate_of.astype(BF16)
    rest = gate_of - high.astype(F32)
    middle = rest.astype(BF16)
    low = (rest - middle.astype(F32)).astype(BF16)
    tok_ref[src, width : width + 4 * GROUP, :] = jnp.concatenate([high, middle, low, jnp.zeros_like(low)], axis=0)
    step = 16
    rows = lax.broadcasted_iota(jnp.int32, (step, tokens), 0).astype(F32).astype(BF16)
    for k in range(GROUP):
        wanted = jnp.broadcast_to(row_of[k : k + 1, :], (step, tokens)).astype(BF16)
        for h in range(capacity // step):
            hit = wanted == rows + jnp.asarray(h * step, BF16)
            start = k * capacity + h * step
            pick_ref[slot, src, start : start + step, :] = jnp.where(hit, jnp.asarray(1, BF16), jnp.asarray(0, BF16))


def build_rows(capacity, src, slot, pick_ref, tok_ref, gate_ref, x_ref):
    width = x_ref.shape[2]
    found = dot(pick_ref[slot, src], tok_ref[src], 1, 1)
    x_ref[src] = found[:, :width].astype(BF16)
    gates = []
    for k in range(GROUP):
        rows = found[k * capacity : (k + 1) * capacity, :]
        gates.append(rows[:, width + k : width + k + 1] + rows[:, width + GROUP + k : width + GROUP + k + 1] + rows[:, width + 2 * GROUP + k : width + 2 * GROUP + k + 1])
    gate = jnp.concatenate(gates, axis=0)
    gate_ref[src] = gate
    return gate


def schedule(groups, sources, begin, wait, dispatch, expert, combine, finish):
    group = pl.program_id(0)

    @pl.when(group == 0)
    def _():
        begin()

        def first(src, carry):
            wait(src)
            dispatch(src)
            return carry

        lax.fori_loop(0, sources, first, 0)

    @pl.when((group > 0) & (group < groups))
    def _():
        def middle(src, carry):
            combine(src)
            dispatch(src)
            return carry

        lax.fori_loop(0, sources, middle, 0)

    @pl.when(group < groups)
    def _():
        def one(k, carry):
            expert(k)
            return carry

        lax.fori_loop(0, GROUP, one, 0, unroll=UNROLL)

    @pl.when(group == groups)
    def _():
        def last(src, carry):
            finish(src)
            return carry

        lax.fori_loop(0, sources, last, 0)


def fwd_kernel(capacity, groups, base_ref, meta_ref, w1_ref, w3_ref, w2_ref, tokens_ref, out_ref, sum_ref, tok_ref, pick_ref, gate_ref, x_ref, o_ref, sem, out_sem):
    group = pl.program_id(0)
    sources = tok_ref.shape[0]
    width = x_ref.shape[2]
    now = group % 2
    before = 1 - now

    def load(src):
        return pltpu.make_async_copy(tokens_ref.at[src], tok_ref.at[src, pl.ds(0, width)], sem.at[src])

    def begin():
        for src in range(sources):
            load(src).start()

    def dispatch(src):
        route(meta_ref, src, base_ref[0] + group * GROUP, capacity, pick_ref, now, tok_ref)
        build_rows(capacity, src, now, pick_ref, tok_ref, gate_ref, x_ref)

    def expert(k):
        here = pl.ds(pl.multiple_of(k * capacity, capacity), capacity)
        x = x_ref[:, here, :].reshape(sources * capacity, width)
        ff = w1_ref.shape[2]
        a = dot(x, jnp.concatenate([w1_ref[k], w3_ref[k]], axis=1), 1, 0)
        hidden = (jax.nn.silu(a[:, :ff]) * a[:, ff:]).astype(BF16)
        out = dot(hidden, w2_ref[k], 1, 1).astype(BF16).astype(F32)
        gate = gate_ref[:, here, :].reshape(sources * capacity, 1)
        o_ref[:, here, :] = (gate * out).reshape(sources, capacity, width)

    def added(src):
        rest = o_ref[src].T
        pick = pick_ref[before, src]
        parts = []
        for _ in range(3):
            parts.append(rest.astype(BF16))
            rest = rest - parts[-1].astype(F32)
        return dot(parts[0], pick, 1, 0) + dot(parts[1], pick, 1, 0) + dot(parts[2], pick, 1, 0)

    def combine(src):
        @pl.when(group == 1)
        def _():
            sum_ref[src] = jnp.zeros(sum_ref.shape[1:], F32)

        sum_ref[src] += added(src)

    def store(src):
        return pltpu.make_async_copy(sum_ref.at[src], out_ref.at[src], out_sem.at[src])

    def finish(src):
        sum_ref[src] += added(src)
        store(src).start()

    schedule(groups, sources, begin, lambda src: load(src).wait(), dispatch, expert, combine, finish)

    @pl.when(group == groups)
    def _():
        for src in range(sources):
            store(src).wait()


def bwd_kernel(layer, capacity, groups, held, pieces, base_ref, meta_ref, w1_ref, w3_ref, w2_ref, tokens_ref, *refs):
    piece_refs, other_refs, refs = refs[:pieces], refs[pieces : pieces + held], refs[pieces + held :]
    out_ref, d1_ref, d3_ref, d2_ref, send_ref, sum_ref, tok_ref, grad_ref, pick_ref, gate_ref, x_ref, g_ref, r_ref, d_ref, sem, grad_sem, out_sem, d_sem = refs[:18]
    d_refs = (d1_ref, d3_ref, d2_ref)
    group = pl.program_id(0)
    sources = tok_ref.shape[0]
    width = x_ref.shape[2]
    now = group % 2
    before = 1 - now

    def load(src):
        return pltpu.make_async_copy(tokens_ref.at[src], tok_ref.at[src, pl.ds(0, width)], sem.at[src])

    def load_grad(src):
        piece = piece_refs[0].at[src] if pieces == 1 else piece_refs[src]
        return pltpu.make_async_copy(piece, grad_ref.at[src], grad_sem.at[src])

    def begin():
        for src in range(sources):
            load(src).start()
            load_grad(src).start()

    def wait(src):
        load(src).wait()
        pltpu.make_async_copy(grad_ref.at[src], grad_ref.at[src], grad_sem.at[src]).wait()

    def dispatch(src):
        route(meta_ref, src, base_ref[0] + group * GROUP, capacity, pick_ref, now, tok_ref)
        gate = build_rows(capacity, src, now, pick_ref, tok_ref, gate_ref, x_ref)
        g_ref[src] = (gate * dot(pick_ref[now, src], grad_ref[src], 1, 1)).astype(BF16)

    def expert(k):
        here = pl.ds(pl.multiple_of(k * capacity, capacity), capacity)
        x = x_ref[:, here, :].reshape(sources * capacity, width)
        g = g_ref[:, here, :].reshape(sources * capacity, width)
        ff = w1_ref.shape[2]
        both = jnp.concatenate([w1_ref[k], w3_ref[k]], axis=1)
        a = dot(x, both, 1, 0)
        a_three = a[:, ff:]
        act, slope = silu_parts(a[:, :ff])
        hidden = (act * a_three).astype(BF16)
        grad_hidden = dot(g, w2_ref[k], 1, 0)
        grad_one = (grad_hidden * a_three * slope).astype(BF16)
        grad_three = (grad_hidden * act).astype(BF16)
        grads = jnp.concatenate([grad_one, grad_three], axis=1)
        r_ref[:, here, :] = dot(grads, both, 1, 1).astype(BF16).reshape(sources, capacity, width)
        d13 = dot(x, grads, 0, 0).astype(BF16)
        d2 = dot(g, hidden, 0, 0).astype(BF16)
        for i, value in enumerate((d13[:, :ff], d13[:, ff:], d2)):
            d_ref[now, i, k] = value

    def added(src):
        return dot(r_ref[src], pick_ref[before, src], 0, 0)

    def combine(src):
        @pl.when(group == 1)
        def _():
            sum_ref[src] = jnp.zeros(sum_ref.shape[1:], F32)

        sum_ref[src] += added(src)

    def store(src):
        return pltpu.make_async_copy(grad_ref.at[src], out_ref.at[src], out_sem.at[src])

    def finish(src):
        grad_ref[src] = (sum_ref[src] + added(src)).astype(BF16)
        store(src).start()

    def experts_at(start, step):
        return pl.ds(pl.multiple_of((start + step) * GROUP, GROUP), GROUP)

    def d_stores(step):
        slot = step % 2
        made = [pltpu.make_async_copy(d_ref.at[slot, i], d_refs[i].at[layer, experts_at(base_ref[1], step)], d_sem.at[slot, i]) for i in range(3)]
        return made + [pltpu.make_async_copy(d_ref.at[slot], send_ref.at[:, experts_at(0, step)], d_sem.at[slot, 3])]

    def other_load(step):
        return pltpu.make_async_copy(other_refs[0].at[:, experts_at(0, step)], refs[18].at[step % 2], refs[19].at[step % 2, 3])

    def other_stores(step):
        slot = step % 2
        return [pltpu.make_async_copy(refs[18].at[slot, i], d_refs[i].at[1 - layer, experts_at(base_ref[2], step)], refs[19].at[slot, i]) for i in range(3)]

    def start_all(copies):
        for copy in copies:
            copy.start()

    def wait_all(copies):
        for copy in copies:
            copy.wait()

    @pl.when(group >= 2)
    def _():
        wait_all(d_stores(group - 2))
        if held:
            wait_all(other_stores(group - 2))

    if held:
        @pl.when(group >= 1)
        def _():
            other_load(group - 1).wait()
            start_all(other_stores(group - 1))

        @pl.when(group < groups)
        def _():
            other_load(group).start()

    schedule(groups, sources, begin, wait, dispatch, expert, combine, finish)

    @pl.when(group < groups)
    def _():
        start_all(d_stores(group))

    @pl.when(group == groups)
    def _():
        wait_all(d_stores(group - 1))
        if held:
            wait_all(other_stores(group - 1))
        for src in range(sources):
            store(src).wait()


def weight_specs(layer, groups, width, ff):
    spec = pl.BlockSpec((None, GROUP, width, ff), lambda g, base: (layer, base[1] + jnp.minimum(g, groups - 1), 0, 0))
    return [spec, spec, spec]


def whole():
    return pl.BlockSpec(memory_space=pltpu.VMEM)


def anywhere():
    return pl.BlockSpec(memory_space=pl.ANY)


def expert_forward(layer, capacity, groups, base, tok, meta, w1, w3, w2):
    sources, width, tokens = tok.shape
    ff = w1.shape[3]
    rows = GROUP * capacity
    return pl.pallas_call(
        functools.partial(fwd_kernel, capacity, groups),
        out_shape=jax.ShapeDtypeStruct((sources, width, tokens), F32),
        grid_spec=pltpu.PrefetchScalarGridSpec(
            num_scalar_prefetch=1,
            grid=(groups + 1,),
            in_specs=[whole()] + weight_specs(layer, groups, width, ff) + [anywhere()],
            out_specs=anywhere(),
            scratch_shapes=[
                pltpu.VMEM((sources, width, tokens), F32),
                pltpu.VMEM((sources, width + 4 * GROUP, tokens), BF16),
                pltpu.VMEM((2, sources, rows, tokens), BF16),
                pltpu.VMEM((sources, rows, 1), F32),
                pltpu.VMEM((sources, rows, width), BF16),
                pltpu.VMEM((sources, rows, width), F32),
                pltpu.SemaphoreType.DMA((sources,)),
                pltpu.SemaphoreType.DMA((sources,)),
            ],
        ),
        compiler_params=pltpu.CompilerParams(vmem_limit_bytes=VMEM_LIMIT),
        cost_estimate=pl.CostEstimate(flops=30_000_000_000, bytes_accessed=30_000_000, transcendentals=0),
    )(base, meta, w1, w3, w2, tok)


def expert_backward(layer, capacity, groups, base, tok, grads, meta, w1, w3, w2, held):
    sources, width, tokens = tok.shape
    ff = w1.shape[3]
    rows = GROUP * capacity
    own = groups * GROUP
    pieces = len(grads)
    grad_shape = jax.ShapeDtypeStruct(w1.shape, BF16)
    block = pltpu.VMEM((2, 3, GROUP, width, ff), BF16)
    more = [block, pltpu.SemaphoreType.DMA((2, 4))] if held else []
    return pl.pallas_call(
        functools.partial(bwd_kernel, layer, capacity, groups, len(held), pieces),
        out_shape=(jax.ShapeDtypeStruct((sources, width, tokens), BF16), grad_shape, grad_shape, grad_shape, jax.ShapeDtypeStruct((3, own, width, ff), BF16)),
        grid_spec=pltpu.PrefetchScalarGridSpec(
            num_scalar_prefetch=1,
            grid=(groups + 1,),
            in_specs=[whole()] + weight_specs(layer, groups, width, ff) + [anywhere()] * (1 + pieces + len(held)),
            out_specs=(anywhere(),) * 5,
            scratch_shapes=[
                pltpu.VMEM((sources, width, tokens), F32),
                pltpu.VMEM((sources, width + 4 * GROUP, tokens), BF16),
                pltpu.VMEM((sources, width, tokens), BF16),
                pltpu.VMEM((2, sources, rows, tokens), BF16),
                pltpu.VMEM((sources, rows, 1), F32),
                pltpu.VMEM((sources, rows, width), BF16),
                pltpu.VMEM((sources, rows, width), BF16),
                pltpu.VMEM((sources, rows, width), BF16),
                block,
                pltpu.SemaphoreType.DMA((sources,)),
                pltpu.SemaphoreType.DMA((sources,)),
                pltpu.SemaphoreType.DMA((sources,)),
                pltpu.SemaphoreType.DMA((2, 4)),
            ]
            + more,
        ),
        input_output_aliases={7 + pieces + i: 1 + i for i in range(len(held) - 1)},
        compiler_params=pltpu.CompilerParams(vmem_limit_bytes=VMEM_LIMIT),
        cost_estimate=pl.CostEstimate(flops=40_000_000_000, bytes_accessed=50_000_000, transcendentals=0),
    )(base, meta, w1, w3, w2, tok, *grads, *held)


def place_kernel(base_ref, recv_ref, *refs):
    for i in range(3):
        refs[3 + i][...] = recv_ref[i]


def place(layer, groups, base, recv, held):
    width, ff = recv.shape[2:]
    few = 8
    spec = pl.BlockSpec((None, few, width, ff), lambda g, base: (layer, base[2] * (GROUP // few) + g, 0, 0))
    shape = jax.ShapeDtypeStruct(held[0].shape, BF16)
    return pl.pallas_call(
        place_kernel,
        out_shape=(shape, shape, shape),
        grid_spec=pltpu.PrefetchScalarGridSpec(
            num_scalar_prefetch=1,
            grid=(groups * GROUP // few,),
            in_specs=[pl.BlockSpec((3, few, width, ff), lambda g, base: (0, g, 0, 0))] + [anywhere()] * 3,
            out_specs=(spec, spec, spec),
        ),
        input_output_aliases={2: 0, 3: 1, 4: 2},
        compiler_params=pltpu.CompilerParams(vmem_limit_bytes=VMEM_LIMIT),
        cost_estimate=pl.CostEstimate(flops=5_000_000_000, bytes_accessed=2 * recv.size * 2, transcendentals=0),
    )(base, recv, *held)


def neighbours():
    ep = lax.axis_index("ep")
    dp = lax.axis_index("dp")
    return ({"ep": ep + 1 - 2 * (ep % 2), "dp": dp}, {"ep": (ep + 2) % 4, "dp": dp}, {"ep": ep, "dp": 1 - dp})


def greet(devices):
    barrier = pltpu.get_barrier_semaphore()
    for device in devices:
        pl.semaphore_signal(barrier, inc=1, device_id=device, device_id_type=pl.DeviceIdType.MESH)
    pl.semaphore_wait(barrier, len(devices))


def gather_kernel(count, *refs):
    own_refs, out_refs, land_refs = refs[:count], refs[count : 2 * count], refs[2 * count : 3 * count]
    send_sem, recv_sem, store_sem = refs[3 * count :]
    by_x, by_y, partner = devices = neighbours()
    greet(devices)
    stores = []

    def copy(which, n, source, target, half, device):
        rows = own_refs[which].shape[0]
        span = pl.ds(0, rows) if half is None else pl.ds(half * (rows // 2), rows // 2)
        block = own_refs[which].at[span] if source == 0 else land_refs[which].at[source, span]
        made = pltpu.make_async_remote_copy(
            src_ref=block,
            dst_ref=land_refs[which].at[target, span],
            send_sem=send_sem.at[which, n],
            recv_sem=recv_sem.at[which, n],
            device_id=device,
            device_id_type=pl.DeviceIdType.MESH,
        )
        made.start()
        return made

    def store(which, slot):
        block = own_refs[which] if slot == 0 else land_refs[which].at[slot]
        made = pltpu.make_async_copy(block, out_refs[which].at[slot], store_sem.at[which, slot])
        made.start()
        stores.append(made)

    made = []
    for which in range(count):
        made.append([
            copy(which, 0, 0, 1, 0, by_x),
            copy(which, 1, 0, 2, 1, by_y),
            copy(which, 2, 0, 1, 1, by_x),
            copy(which, 3, 0, 2, 0, by_y),
            copy(which, 4, 0, 4, None, partner),
        ])
        store(which, 0)
    for which in range(count):
        steps = made[which]
        steps[0].wait_recv()
        steps.append(copy(which, 5, 1, 3, 0, by_y))
        steps[1].wait_recv()
        steps.append(copy(which, 6, 2, 3, 1, by_x))
        steps[2].wait_recv()
        steps.append(copy(which, 7, 1, 5, None, partner))
        store(which, 1)
        steps[3].wait_recv()
        steps.append(copy(which, 8, 2, 6, None, partner))
        store(which, 2)
        steps[4].wait_recv()
        store(which, 4)
    for which in range(count):
        steps = made[which]
        steps[5].wait_recv()
        steps.append(copy(which, 9, 3, 7, 0, partner))
        steps[6].wait_recv()
        steps.append(copy(which, 10, 3, 7, 1, partner))
        store(which, 3)
    for which in range(count):
        steps = made[which]
        steps[7].wait_recv()
        store(which, 5)
        steps[8].wait_recv()
        store(which, 6)
        steps[9].wait_recv()
        steps[10].wait_recv()
        store(which, 7)
        for n in range(11):
            steps[n].wait_send()
    for made_store in stores:
        made_store.wait()


def gather_tokens(cid, arrays):
    count = len(arrays)
    out = pl.pallas_call(
        functools.partial(gather_kernel, count),
        out_shape=tuple(jax.ShapeDtypeStruct((8,) + x.shape, x.dtype) for x in arrays),
        in_specs=[whole()] * count,
        out_specs=(anywhere(),) * count,
        scratch_shapes=[pltpu.VMEM((8,) + x.shape, x.dtype) for x in arrays] + [pltpu.SemaphoreType.DMA((count, n)) for n in (11, 11, 8)],
        compiler_params=pltpu.CompilerParams(collective_id=cid, has_side_effects=True, vmem_limit_bytes=VMEM_LIMIT),
        cost_estimate=pl.CostEstimate(flops=10_000_000_000, bytes_accessed=10_000_000, transcendentals=0),
    )(*arrays)
    return out


def reduce_kernel(extra, part_ref, *refs):
    extra_ref, refs = refs[:extra], refs[extra:]
    (out_ref, *other_ref), refs = refs[: 1 + extra], refs[1 + extra :]
    mine_ref, pair_ref, stage_ref, relay_ref, last_ref, send_sem, recv_sem, load_sem = refs
    devices = neighbours()
    by_x, by_y, partner = devices
    greet(devices)
    rows = part_ref.shape[1]
    half = rows // 2
    low, high, full = pl.ds(0, half), pl.ds(half, half), pl.ds(0, rows)
    wire = part_ref.dtype

    def copy(n, source, target, device):
        made = pltpu.make_async_remote_copy(
            src_ref=source,
            dst_ref=target,
            send_sem=send_sem.at[n],
            recv_sem=recv_sem.at[n],
            device_id=device,
            device_id_type=pl.DeviceIdType.MESH,
        )
        made.start()
        return made

    def chip_sum(i, span):
        return mine_ref[i, span, :].astype(F32) + pair_ref[i, span, :].astype(F32)

    loads = {}
    for i in (3, 1, 2, 0):
        loads[i] = pltpu.make_async_copy(part_ref.at[i], mine_ref.at[i], load_sem.at[i])
        loads[i].start()
    steps = {i: copy(i, part_ref.at[4 + i], pair_ref.at[i], partner) for i in (3, 1, 2, 0)}
    loads[3].wait()
    steps[3].wait_recv()
    stage_ref[0, low, :] = chip_sum(3, low).astype(wire)
    steps[4] = copy(4, stage_ref.at[0, low], relay_ref.at[0], by_x)
    stage_ref[0, high, :] = chip_sum(3, high).astype(wire)
    steps[5] = copy(5, stage_ref.at[0, high], relay_ref.at[1], by_y)
    loads[1].wait()
    steps[1].wait_recv()
    stage_ref[1, low, :] = chip_sum(1, low).astype(wire)
    steps[6] = copy(6, stage_ref.at[1, low], last_ref.at[0, low], by_x)
    loads[2].wait()
    steps[2].wait_recv()
    stage_ref[2, high, :] = chip_sum(2, high).astype(wire)
    steps[7] = copy(7, stage_ref.at[2, high], last_ref.at[1, high], by_y)
    if extra:
        for i in range(3):
            steps[10 + i] = copy(10 + i, extra_ref[0].at[i], other_ref[0].at[i], partner)
    steps[5].wait_recv()
    stage_ref[1, high, :] = (chip_sum(1, high) + relay_ref[1].astype(F32)).astype(wire)
    steps[8] = copy(8, stage_ref.at[1, high], last_ref.at[0, high], by_x)
    steps[4].wait_recv()
    stage_ref[2, low, :] = (chip_sum(2, low) + relay_ref[0].astype(F32)).astype(wire)
    steps[9] = copy(9, stage_ref.at[2, low], last_ref.at[1, low], by_y)
    loads[0].wait()
    steps[0].wait_recv()
    out_ref[...] = chip_sum(0, full)
    steps[6].wait_recv()
    steps[7].wait_recv()
    steps[8].wait_recv()
    steps[9].wait_recv()
    out_ref[...] += last_ref[0].astype(F32) + last_ref[1].astype(F32)
    for n in range(10, 10 + 3 * extra):
        steps[n].wait_recv()
    for n in range(10 + 3 * extra):
        steps[n].wait_send()


def reduce_tokens(cid, part, *extra):
    rows, tokens = part.shape[1:]
    out = pl.pallas_call(
        functools.partial(reduce_kernel, len(extra)),
        out_shape=(jax.ShapeDtypeStruct((rows, tokens), F32),) + tuple(jax.ShapeDtypeStruct(x.shape, x.dtype) for x in extra),
        in_specs=[anywhere()] * (1 + len(extra)),
        out_specs=(whole(),) + (anywhere(),) * len(extra),
        scratch_shapes=[
            pltpu.VMEM((4, rows, tokens), part.dtype),
            pltpu.VMEM((4, rows, tokens), part.dtype),
            pltpu.VMEM((3, rows, tokens), part.dtype),
            pltpu.VMEM((2, rows // 2, tokens), part.dtype),
            pltpu.VMEM((2, rows, tokens), part.dtype),
            pltpu.SemaphoreType.DMA((13,)),
            pltpu.SemaphoreType.DMA((13,)),
            pltpu.SemaphoreType.DMA((4,)),
        ],
        compiler_params=pltpu.CompilerParams(collective_id=cid, has_side_effects=True, vmem_limit_bytes=VMEM_LIMIT),
        cost_estimate=pl.CostEstimate(flops=10_000_000_000, bytes_accessed=10_000_000, transcendentals=0),
    )(part, *extra)
    return out if extra else out[0]


def send_over(x, flip):
    return lax.ppermute(x, "ep", [(i, i ^ flip) for i in range(4)])


def swap_cores(x):
    return lax.ppermute(x, "dp", [(0, 1), (1, 0)])


def sum_start(x):
    half = x.shape[0] // 2
    dp = lax.axis_index("dp")
    mine = lax.dynamic_slice_in_dim(x, dp * half, half, 0)
    other = lax.dynamic_slice_in_dim(x, (1 - dp) * half, half, 0)
    chip = (mine.astype(F32) + swap_cores(other).astype(F32)).astype(BF16)
    sent = [chip]
    for flip in (1, 2, 3):
        sent.append(send_over(chip, flip))
    return sent


def sum_finish(parts):
    total = sum(part.astype(F32) for part in parts).astype(BF16)
    other = swap_cores(total)
    first = lax.axis_index("dp") == 0
    return jnp.concatenate([jnp.where(first, total, other), jnp.where(first, other, total)], axis=0)


def dense_forward(act, w_dense, ws_gate, ws_up):
    mixed = (act.astype(F32) + dot(w_dense, act, 0, 0)).astype(BF16)
    s_one = dot(ws_gate, mixed, 0, 0)
    s_three = dot(ws_up, mixed, 0, 0)
    shared_hidden = (jax.nn.silu(s_one) * s_three).astype(BF16)
    return mixed, s_one, s_three, shared_hidden


def shared_backward(grad_y, saved, ws_gate, ws_up, ws_down):
    mixed, s_one, s_three, shared_hidden = saved
    act_one, slope = silu_parts(s_one)
    grad_shared = dot(ws_down, grad_y, 1, 0)
    grad_s_one = (grad_shared * s_three * slope).astype(BF16)
    grad_s_three = (grad_shared * act_one).astype(BF16)
    g_ws_down = dot(grad_y, shared_hidden, 1, 1).astype(BF16)
    g_ws_gate = dot(mixed, grad_s_one, 1, 1).astype(BF16)
    g_ws_up = dot(mixed, grad_s_three, 1, 1).astype(BF16)
    back = dot(ws_gate, grad_s_one, 1, 0) + dot(ws_up, grad_s_three, 1, 0)
    return back, [g_ws_gate, g_ws_up, g_ws_down]


def dense_finish(grad_y, routed, shared, act, w_dense):
    grad_mixed = (grad_y.astype(F32) + routed + shared).astype(BF16)
    grad_act = (grad_mixed.astype(F32) + dot(w_dense, grad_mixed, 1, 0)).astype(BF16)
    return grad_act, dot(act, grad_mixed, 1, 1).astype(BF16)


def dense_backward(grad_y, routed, saved, act, w_dense, ws_gate, ws_up, ws_down):
    back, parts = shared_backward(grad_y, saved, ws_gate, ws_up, ws_down)
    grad_act, g_w_dense = dense_finish(grad_y, routed, back, act, w_dense)
    return grad_act, [g_w_dense] + parts


def solution(mesh):
    ep_size = mesh.shape["ep"]
    dp_size = mesh.shape["dp"]
    tok_spec = P(ALL_AXES, None)
    route_spec = P(None, ALL_AXES, None)
    exp_spec = P(None, "ep", None, None)
    repl_spec = P(None, None, None)

    def body(act_in, grad_out, slot_ids, gate_vals, w_dense, w_gate, w_up, w_down, ws_gate, ws_up, ws_down):
        layers, local_exp = w_gate.shape[:2]
        tokens = act_in.shape[0]
        top = slot_ids.shape[2]
        own = local_exp // dp_size
        groups = own // GROUP
        capacity = 2 * tokens * top // (local_exp * ep_size)
        dp = lax.axis_index("dp")
        base = jnp.stack([lax.axis_index("ep") * local_exp + dp * own, dp * groups, (dp_size - 1 - dp) * groups]).astype(jnp.int32)
        w_down_t = jnp.swapaxes(w_down, 2, 3)
        meta = jnp.concatenate([jnp.swapaxes(slot_ids, 1, 2).astype(F32), jnp.swapaxes(gate_vals, 1, 2)], axis=1)
        meta = meta.reshape(layers * 2 * top, tokens)

        x1 = act_in.T
        grad_y2 = grad_out.T
        saved1 = dense_forward(x1, w_dense[0], ws_gate[0], ws_up[0])
        tok1, metas = gather_tokens(0, [saved1[0], meta])
        tok1, grad_y2 = lax.optimization_barrier((tok1, grad_y2))
        grads2 = [grad_y2, send_over(grad_y2, 1), send_over(grad_y2, 2), send_over(grad_y2, 3)]
        grads2 = grads2 + [swap_cores(x) for x in grads2]
        meta1, meta2 = metas[:, : 2 * top], metas[:, 2 * top :]
        part = expert_forward(0, capacity, groups, base, tok1, meta1, w_gate, w_up, w_down_t)
        routed = reduce_tokens(1, part)
        x2 = (saved1[0].astype(F32) + routed + dot(ws_down[0], saved1[3], 0, 0)).astype(BF16)
        saved2 = dense_forward(x2, w_dense[1], ws_gate[1], ws_up[1])
        (tok2,) = gather_tokens(2, [saved2[0]])
        back2, *held, send2 = expert_backward(1, capacity, groups, base, tok2, grads2, meta2, w_gate, w_up, w_down_t, [])
        routed2, recv2 = reduce_tokens(3, back2, send2)
        grad_y1, dense2 = dense_backward(grad_y2, routed2, saved2, x2, w_dense[1], ws_gate[1], ws_up[1], ws_down[1])
        (grad1_all,) = gather_tokens(4, [grad_y1])
        shared1, parts1 = shared_backward(grad_y1, saved1, ws_gate[0], ws_up[0], ws_down[0])
        ff = ws_gate.shape[2]
        width = w_dense.shape[1]
        early = jnp.concatenate(dense2 + parts1 + [jnp.zeros((width, -(width + 6 * ff) % 128), BF16)], axis=1)
        early = sum_start(early)
        tok1, early[0] = lax.optimization_barrier((tok1, early[0]))
        back1, *held, send1 = expert_backward(0, capacity, groups, base, tok1, [grad1_all], meta1, w_gate, w_up, w_down_t, [recv2] + held)
        routed1, recv1 = reduce_tokens(5, back1, send1)
        grad_x, g_w_dense1 = dense_finish(grad_y1, routed1, shared1, x1, w_dense[0])
        late = sum_start(g_w_dense1)
        g_gate, g_up, g_down = place(0, groups, base, recv1, held)
        g_gate, late = lax.optimization_barrier((g_gate, late))
        g_down = jnp.swapaxes(g_down, 2, 3)
        early = sum_finish(early)
        late = sum_finish(late)
        g_dense = jnp.stack([late, early[:, :width]])
        shared = [jnp.stack([early[:, width + (3 + i) * ff : width + (4 + i) * ff], early[:, width + i * ff : width + (i + 1) * ff]]) for i in range(3)]
        return (grad_x.T, g_dense, g_gate, g_up, g_down, shared[0], shared[1], jnp.swapaxes(shared[2], 1, 2))

    return jax.shard_map(body, mesh=mesh, in_specs=(tok_spec, tok_spec, route_spec, route_spec, repl_spec, exp_spec, exp_spec, exp_spec, repl_spec, repl_spec, repl_spec), out_specs=(tok_spec, repl_spec, exp_spec, exp_spec, exp_spec, repl_spec, repl_spec, repl_spec), check_vma=False)
```

profile of v0, /device:TPU:0, one launch (start us, length us, event | category | flops | bytes accessed | tf_op | source)
XLA Modules:
  0.0 505.7 jit_solution(10373833241589314407)
XLA Ops:
  0.6 0.8 convert_bitcast_fusion
  1.5 2.9 fusion.9.refs_0_
  4.3 0.6 pad_maximum_fusion.4
  5.0 34.2 %shard_map.170 = (bf16[8,448,768]{2,1,0:T(8,128)(2,1)}, f32[8,32,768]{2,1,0:T(8,128)}) custom-call(bf16[448,768]{1,0:T(8,128)(2,1)} %fusion.9.refs_0_, f32[32,768]{1,0:T(8,128)} %bitcast.164), custom_call_target="tpu_custom_call" | custom-call | flops 10000000000 | bytes 10000000 | tf_op jit(solution)/shard_map/pallas_call | solution.py:485
  39.2 1.0 collective-permute-start
  40.2 1.1 collective-permute-start.1
  41.2 1.5 collective-permute-start.2
  43.1 1.0 fusion.64
  44.1 0.7 pad_add_fusion.base_ref
  44.8 73.6 %shard_map.171.part_ref = f32[8,448,768]{2,1,0:T(8,128)} custom-call(s32[3]{0:T(128)} %pad_add_fusion.base_ref, f32[8,16,768]{2,1,0:T(8,128)} %get-tuple-element.75.meta_ref, bf16[2,96,448,128]{3,2,1,0:T(8,128)(2,1)} %w1_ref.5, bf16[2,96,448,128]{3,2,1,0:T(8,128)(2,1)} %w3_ref.5, bf16[2,96,448,128]{3,2,1,0:T(8,128)(2,1)} %bitcast.161, ...), custom_call_target="tpu_custom_call" | custom-call | flops 30000001024 | bytes 30000000 | tf_op jit(solution)/shard_map/pallas_call | solution.py:307
  118.4 52.2 %shard_map.172 = f32[448,768]{1,0:T(8,128)} custom-call(f32[8,448,768]{2,1,0:T(8,128)} %shard_map.171.part_ref), custom_call_target="tpu_custom_call" | custom-call | flops 10000000000 | bytes 10000000 | tf_op jit(solution)/shard_map/pallas_call | solution.py:568
  170.7 1.2 multiply_convert_fusion.5
  172.4 0.8 copy-done.21
  173.3 0.6 fusion.12.refs_0_
  174.7 1.5 multiply_convert_fusion.3
  176.2 2.1 convolution_convert_fusion.5
  178.4 1.0 convolution_convert_fusion.7
  179.4 1.0 convolution_convert_fusion.6
  180.7 1.4 fusion.1
  182.7 28.7 %shard_map.173.tokens_ref = bf16[8,448,768]{2,1,0:T(8,128)(2,1)} custom-call(bf16[448,768]{1,0:T(8,128)(2,1)} %copy-done.1), custom_call_target="tpu_custom_call" | custom-call | flops 10000000000 | bytes 10000000 | tf_op jit(solution)/shard_map/pallas_call | solution.py:485
  211.4 68.1 %shard_map.174 = (bf16[8,448,768]{2,1,0:T(8,128)(2,1)}, bf16[2,96,448,128]{3,2,1,0:T(8,128)(2,1)}, bf16[2,96,448,128]{3,2,1,0:T(8,128)(2,1)}, bf16[2,96,448,128]{3,2,1,0:T(8,128)(2,1)}, bf16[3,48,448,128]{3,2,1,0:T(8,128)(2,1)}) custom-call(s32[3]{0:T(128)} %pad_add_fusion.base_ref, f32[8,16,768]{2,1,0:T(8,128)} %get-tuple-element.74.meta_ref, ...), custom_call_target="tpu_custom_call" | custom-call | flops 40000000000 | bytes 50000000 | tf_op jit(solution)/shard_map/pallas_call | solution.py:340
  279.6 31.6 %shard_map.175 = (f32[448,768]{1,0:T(8,128)}, bf16[3,48,448,128]{3,2,1,0:T(8,128)(2,1)}) custom-call(bf16[8,448,768]{2,1,0:T(8,128)(2,1)} %get-tuple-element.40.part_ref, bf16[3,48,448,128]{3,2,1,0:T(8,128)(2,1)} %get-tuple-element.41.refs_0_), custom_call_target="tpu_custom_call" | custom-call | flops 10000000000 | bytes 10000000 | tf_op jit(solution)/shard_map/pallas_call | solution.py:568
  311.2 2.2 add_convert_fusion
  314.0 0.5 convolution_convert_fusion.1
  316.9 2.2 concatenate.13
  319.2 0.9 constant_dynamic-slice_fusion
  320.4 28.1 %shard_map.176.refs_0_ = bf16[8,448,768]{2,1,0:T(8,128)(2,1)} custom-call(bf16[448,768]{1,0:T(8,128)(2,1)} %copy-done.2), custom_call_target="tpu_custom_call" | custom-call | flops 10000000000 | bytes 10000000 | tf_op jit(solution)/shard_map/pallas_call | solution.py:485
  348.5 1.4 fusion.43
  350.0 2.0 add_convert_fusion.2
  352.0 69.9 %shard_map.177 = (bf16[8,448,768]{2,1,0:T(8,128)(2,1)}, bf16[2,96,448,128]{3,2,1,0:T(8,128)(2,1)}, bf16[2,96,448,128]{3,2,1,0:T(8,128)(2,1)}, bf16[2,96,448,128]{3,2,1,0:T(8,128)(2,1)}, bf16[3,48,448,128]{3,2,1,0:T(8,128)(2,1)}) custom-call(s32[3]{0:T(128)} %pad_add_fusion.base_ref, ...), custom_call_target="tpu_custom_call", output_to_operand_aliasing={{1}: (8, {}), {2}: (9, {}), {3}: (10, {})} | custom-call | flops 40000000000 | bytes 50000000 | tf_op jit(solution)/shard_map/pallas_call | solution.py:340
  421.9 32.0 %shard_map.178 = (f32[448,768]{1,0:T(8,128)}, bf16[3,48,448,128]{3,2,1,0:T(8,128)(2,1)}) custom-call(bf16[8,448,768]{2,1,0:T(8,128)(2,1)} %get-tuple-element.48.part_ref, bf16[3,48,448,128]{3,2,1,0:T(8,128)(2,1)} %get-tuple-element.49.refs_0_), custom_call_target="tpu_custom_call" | custom-call | flops 10000000000 | bytes 10000000 | tf_op jit(solution)/shard_map/pallas_call | solution.py:568
  453.9 2.2 fusion.7
  457.1 1.1 collective-permute-done.8
  458.3 1.0 collective-permute-start.9
  459.3 1.5 collective-permute-start.15
  460.7 1.1 collective-permute-start.14
  461.8 1.0 collective-permute-start.13
  462.8 1.1 collective-permute-start.10
  463.8 3.0 collective-permute-done.9
  466.8 1.5 collective-permute-start.11
  468.3 13.2 %shard_map.179 = (bf16[2,96,448,128]{3,2,1,0:T(8,128)(2,1)}, bf16[2,96,448,128]{3,2,1,0:T(8,128)(2,1)}, bf16[2,96,448,128]{3,2,1,0:T(8,128)(2,1)}) custom-call(s32[3]{0:T(128)} %pad_add_fusion.base_ref, bf16[3,48,448,128]{3,2,1,0:T(8,128)(2,1)} %get-tuple-element.51.recv_ref, ...), custom_call_target="tpu_custom_call", output_to_operand_aliasing={{0}: (2, {}), {1}: (3, {}), {2}: (4, {})} | custom-call | flops 5000000000 | bytes 33030144 | tf_op jit(solution)/shard_map/pallas_call | solution.py:381
  481.5 16.2 %collective-permute-done.10 = bf16[224,448]{1,0:T(8,128)(2,1)} collective-permute-done((bf16[224,448]{1,0:T(8,128)(2,1)S(1)}, bf16[224,448]{1,0:T(8,128)(2,1)}, u32[]{:S(2)}, u32[]{:S(2)}) %collective-permute-start.10) | collective-permute-done | bytes 200736 | tf_op jit(solution)/shard_map/ppermute | solution.py:590
  497.7 1.2 add_convert_fusion.3
  498.9 1.8 add_convert_fusion.1
  501.1 1.4 fusion.13
  503.1 1.0 pad_maximum_fusion
  504.1 0.7 maximum_bitcast_fusion.1
  504.9 0.8 pad_maximum_fusion.1
  (92 shorter events, 8.1 us)
Async XLA Ops:
  0.6 3.7 copy-start.20
  5.0 37.7 %copy-start = (bf16[448,768]{1,0:T(8,128)(2,1)S(1)}, bf16[448,768]{1,0:T(8,128)(2,1)}, u32[]{:S(2)}) copy-start(bf16[448,768]{1,0:T(8,128)(2,1)} %fusion.9.refs_0_) | copy-start | bytes 2064388
  5.0 37.7 %copy-start.6 = (bf16[2,448,128]{2,1,0:T(8,128)(2,1)S(1)}, bf16[2,448,128]{2,1,0:T(8,128)(2,1)}, u32[]{:S(2)}) copy-start(bf16[2,448,128]{2,1,0:T(8,128)(2,1)} %param.19) | copy-start | bytes 688132
  39.2 4.0 copy-start.8
  39.2 143.0 %collective-permute-start = (bf16[448,768]{1,0:T(8,128)(2,1)}, bf16[448,768]{1,0:T(8,128)(2,1)}, u32[]{:S(2)}, u32[]{:S(2)}) collective-permute-start(bf16[448,768]{1,0:T(8,128)(2,1)} %bitcast.5.refs_0_), channel_id=1, source_target_pairs={{0,2},{2,0},{4,6},{6,4},{1,3},{3,1},{5,7},{7,5}} | collective-permute-start | bytes 2064392 | tf_op jit(solution)/shard_map/ppermute | solution.py:590
  40.2 142.0 %collective-permute-start.1 = (bf16[448,768]{1,0:T(8,128)(2,1)}, bf16[448,768]{1,0:T(8,128)(2,1)}, u32[]{:S(2)}, u32[]{:S(2)}) collective-permute-start(bf16[448,768]{1,0:T(8,128)(2,1)} %bitcast.5.refs_0_), channel_id=1, source_target_pairs={{0,4},{2,6},{4,0},{6,2},{1,5},{3,7},{5,1},{7,3}} | collective-permute-start | bytes 2064392 | tf_op jit(solution)/shard_map/ppermute | solution.py:590
  41.2 141.4 %collective-permute-start.2 = (bf16[448,768]{1,0:T(8,128)(2,1)}, bf16[448,768]{1,0:T(8,128)(2,1)}, u32[]{:S(2)}, u32[]{:S(2)}) collective-permute-start(bf16[448,768]{1,0:T(8,128)(2,1)} %bitcast.5.refs_0_), channel_id=1, source_target_pairs={{0,6},{2,4},{4,2},{6,0},{1,7},{3,5},{5,3},{7,1}} | collective-permute-start | bytes 2064392 | tf_op jit(solution)/shard_map/ppermute | solution.py:590
  42.7 168.7 %collective-permute-start.3 = (bf16[448,768]{1,0:T(8,128)(2,1)}, bf16[448,768]{1,0:T(8,128)(2,1)}, u32[]{:S(2)}, u32[]{:S(2)}) collective-permute-start(bf16[448,768]{1,0:T(8,128)(2,1)} %bitcast.5.refs_0_), channel_id=1, source_target_pairs={{0,1},{1,0},{2,3},{3,2},{4,5},{5,4},{6,7},{7,6}} | collective-permute-start | bytes 2064392 | tf_op jit(solution)/shard_map/ppermute | solution.py:594
  43.1 127.5 %copy-start.15 = (f32[128,768]{0,1:T(8,128)}, f32[128,768]{0,1:T(8,128)S(1)}, u32[]{:S(2)}) copy-start(f32[128,768]{0,1:T(8,128)S(1)} %convolution_bitcast_fusion.9) | copy-start | bytes 1179652
  118.4 52.2 %copy-start.11 = (bf16[2,448,128]{2,1,0:T(8,128)(2,1)S(1)}, bf16[2,448,128]{2,1,0:T(8,128)(2,1)}, u32[]{:S(2)}) copy-start(bf16[2,448,128]{2,1,0:T(8,128)(2,1)} %param.20) | copy-start | bytes 688132
  170.7 1.3 copy-start.5
  170.7 1.4 copy-start.18
  172.1 1.2 copy-start.21
  173.8 5.5 %copy-start.1 = (bf16[448,768]{1,0:T(8,128)(2,1)}, bf16[448,768]{1,0:T(8,128)(2,1)S(1)}, u32[]{:S(2)}) copy-start(bf16[448,768]{1,0:T(8,128)(2,1)S(1)} %fusion.12.refs_0_) | copy-start | bytes 2064388
  182.2 29.2 %collective-permute-start.4 = (bf16[448,768]{1,0:T(8,128)(2,1)}, bf16[448,768]{1,0:T(8,128)(2,1)}, u32[]{:S(2)}, u32[]{:S(2)}) collective-permute-start(bf16[448,768]{1,0:T(8,128)(2,1)} %collective-permute-done.refs_1_), channel_id=1, source_target_pairs={{0,1},{1,0},{2,3},{3,2},{4,5},{5,4},{6,7},{7,6}} | collective-permute-start | bytes 2064392 | tf_op jit(solution)/shard_map/ppermute | solution.py:594
  182.2 29.2 %collective-permute-start.5 = (bf16[448,768]{1,0:T(8,128)(2,1)}, bf16[448,768]{1,0:T(8,128)(2,1)}, u32[]{:S(2)}, u32[]{:S(2)}) collective-permute-start(bf16[448,768]{1,0:T(8,128)(2,1)} %collective-permute-done.1.refs_2_), channel_id=1, source_target_pairs={{0,1},{1,0},{2,3},{3,2},{4,5},{5,4},{6,7},{7,6}} | collective-permute-start | bytes 2064392 | tf_op jit(solution)/shard_map/ppermute | solution.py:594
  182.7 28.8 %collective-permute-start.6 = (bf16[448,768]{1,0:T(8,128)(2,1)}, bf16[448,768]{1,0:T(8,128)(2,1)}, u32[]{:S(2)}, u32[]{:S(2)}) collective-permute-start(bf16[448,768]{1,0:T(8,128)(2,1)} %collective-permute-done.2.refs_3_), channel_id=1, source_target_pairs={{0,1},{1,0},{2,3},{3,2},{4,5},{5,4},{6,7},{7,6}} | collective-permute-start | bytes 2064392 | tf_op jit(solution)/shard_map/ppermute | solution.py:594
  311.2 2.2 copy-start.22
  313.9 0.9 copy-start.2
  314.0 1.2 copy-start.16
  314.0 1.3 copy-start.19
  314.0 1.5 copy-start.25
  315.9 0.8 copy-start.9
  315.9 1.0 copy-start.13
  315.9 1.0 copy-start.14
  315.9 1.1 copy-start.17
  320.0 28.5 %copy-start.7 = (bf16[2,448,128]{2,1,0:T(8,128)(2,1)S(1)}, bf16[2,448,128]{2,1,0:T(8,128)(2,1)}, u32[]{:S(2)}) copy-start(bf16[2,448,128]{2,1,0:T(8,128)(2,1)} %param.19) | copy-start | bytes 688132
  320.0 28.5 %copy-start.10 = (bf16[128,768]{0,1:T(8,128)(2,1)S(1)}, bf16[128,768]{0,1:T(8,128)(2,1)}, u32[]{:S(2)}) copy-start(bf16[128,768]{0,1:T(8,128)(2,1)} %copy-done.9) | copy-start | bytes 589828
  320.0 30.0 %collective-permute-start.7 = (bf16[224,1280]{1,0:T(8,128)(2,1)}, bf16[224,1280]{1,0:T(8,128)(2,1)}, u32[]{:S(2)}, u32[]{:S(2)}) collective-permute-start(bf16[224,1280]{1,0:T(8,128)(2,1)} %constant_dynamic-slice_fusion), channel_id=1, source_target_pairs={{0,1},{1,0},{2,3},{3,2},{4,5},{5,4},{6,7},{7,6}} | collective-permute-start | bytes 1720328 | tf_op jit(solution)/shard_map/ppermute | solution.py:594
  421.9 32.0 %copy-start.3 = (bf16[448,768]{1,0:T(8,128)(2,1)S(1)}, bf16[448,768]{1,0:T(8,128)(2,1)}, u32[]{:S(2)}) copy-start(bf16[448,768]{1,0:T(8,128)(2,1)} %copy-done.2) | copy-start | bytes 2064388
  421.9 32.0 %copy-start.12 = (bf16[2,448,128]{2,1,0:T(8,128)(2,1)S(1)}, bf16[2,448,128]{2,1,0:T(8,128)(2,1)}, u32[]{:S(2)}) copy-start(bf16[2,448,128]{2,1,0:T(8,128)(2,1)} %param.20) | copy-start | bytes 688132
  453.9 2.2 copy-start.24
  456.1 3.2 copy-start.4
  456.7 1.5 collective-permute-start.8
  458.3 8.5 %collective-permute-start.9 = (bf16[224,448]{1,0:T(8,128)(2,1)S(1)}, bf16[224,448]{1,0:T(8,128)(2,1)S(1)}, u32[]{:S(2)}, u32[]{:S(2)}) collective-permute-start(bf16[224,448]{1,0:T(8,128)(2,1)S(1)} %fusion.16), channel_id=1, source_target_pairs={{0,2},{2,0},{4,6},{6,4},{1,3},{3,1},{5,7},{7,5}} | collective-permute-start | bytes 602120 | tf_op jit(solution)/shard_map/ppermute | solution.py:590
  459.3 39.6 %collective-permute-start.15 = (bf16[224,1280]{1,0:T(8,128)(2,1)S(1)}, bf16[224,1280]{1,0:T(8,128)(2,1)}, u32[]{:S(2)}, u32[]{:S(2)}) collective-permute-start(bf16[224,1280]{1,0:T(8,128)(2,1)S(1)} %copy-done.4), channel_id=1, source_target_pairs={{0,6},{2,4},{4,2},{6,0},{1,7},{3,5},{5,3},{7,1}} | collective-permute-start | bytes 1720328 | tf_op jit(solution)/shard_map/ppermute | solution.py:590
  460.7 38.2 %collective-permute-start.14 = (bf16[224,1280]{1,0:T(8,128)(2,1)S(1)}, bf16[224,1280]{1,0:T(8,128)(2,1)}, u32[]{:S(2)}, u32[]{:S(2)}) collective-permute-start(bf16[224,1280]{1,0:T(8,128)(2,1)S(1)} %copy-done.4), channel_id=1, source_target_pairs={{0,4},{2,6},{4,0},{6,2},{1,5},{3,7},{5,1},{7,3}} | collective-permute-start | bytes 1720328 | tf_op jit(solution)/shard_map/ppermute | solution.py:590
  461.8 37.1 %collective-permute-start.13 = (bf16[224,1280]{1,0:T(8,128)(2,1)S(1)}, bf16[224,1280]{1,0:T(8,128)(2,1)}, u32[]{:S(2)}, u32[]{:S(2)}) collective-permute-start(bf16[224,1280]{1,0:T(8,128)(2,1)S(1)} %copy-done.4), channel_id=1, source_target_pairs={{0,2},{2,0},{4,6},{6,4},{1,3},{3,1},{5,7},{7,5}} | collective-permute-start | bytes 1720328 | tf_op jit(solution)/shard_map/ppermute | solution.py:590
  462.8 34.9 %collective-permute-start.10 = (bf16[224,448]{1,0:T(8,128)(2,1)S(1)}, bf16[224,448]{1,0:T(8,128)(2,1)}, u32[]{:S(2)}, u32[]{:S(2)}) collective-permute-start(bf16[224,448]{1,0:T(8,128)(2,1)S(1)} %fusion.16), channel_id=1, source_target_pairs={{0,4},{2,6},{4,0},{6,2},{1,5},{3,7},{5,1},{7,3}} | collective-permute-start | bytes 602120 | tf_op jit(solution)/shard_map/ppermute | solution.py:590
  466.8 30.9 %collective-permute-start.11 = (bf16[224,448]{1,0:T(8,128)(2,1)S(1)}, bf16[224,448]{1,0:T(8,128)(2,1)}, u32[]{:S(2)}, u32[]{:S(2)}) collective-permute-start(bf16[224,448]{1,0:T(8,128)(2,1)S(1)} %fusion.16), channel_id=1, source_target_pairs={{0,6},{2,4},{4,2},{6,0},{1,7},{3,5},{5,3},{7,1}} | collective-permute-start | bytes 602120 | tf_op jit(solution)/shard_map/ppermute | solution.py:590
  498.8 2.3 copy-start.23
  498.9 3.6 collective-permute-start.12
  500.7 2.0 collective-permute-start.16
where the time goes:
time: 506 us
  Pallas kernels  432 us (85%)
  matrix products  21.7 us (4%)
  waiting for transfers between devices  20.4 us (4%)
  other arithmetic  12.3 us (2%)
  starting transfers between devices  12.3 us (2%)
  local copies, waits for them, and re-layouts  6.07 us (1%)
    pallas_call x2, Pallas kernels, expert_backward(): pl.pallas_call(functools.partial(bwd_kernel, layer, capacity, groups, len...  138 us
    pallas_call x3, Pallas kernels, reduce_tokens(): pl.pallas_call(functools.partial(reduce_kernel, len(extra)), out_shape=(j...  116 us
    pallas_call x3, Pallas kernels, gather_tokens(): pl.pallas_call(functools.partial(gather_kernel, count), out_shape=tuple((...  91 us
    pallas_call x1, Pallas kernels, expert_forward(): pl.pallas_call(functools.partial(fwd_kernel, capacity, groups), out_shape...  73.6 us
    dot_general x23, matrix products, dot(): lax.dot_general(left, right, (((left_dim,), (right_dim,)), ((), ())), pre...  21.7 us
    ppermute x9, waiting for transfers between devices, send_over(): return lax.ppermute(x, 'ep', [(i, i ^ flip) for i in range(4)])  19.2 us
    pallas_call x1, Pallas kernels, place(): pl.pallas_call(place_kernel, out_shape=(shape, shape, shape), grid_spec=p...  13.2 us
    ppermute x9, starting transfers between devices, send_over(): return lax.ppermute(x, 'ep', [(i, i ^ flip) for i in range(4)])  10.5 us
  transfers between devices with their start and end apart: 17, of which 4 were waited for; matrix products, arithmetic and copies ran while one was open for 4% of the time, Pallas kernels for 39%

commit v1 on v0

v1 whole, which is shorter than its diff:
```python
import functools
import jax
import jax.numpy as jnp
from jax import lax
from jax.experimental import pallas as pl
from jax.experimental.pallas import tpu as pltpu
from jax.sharding import PartitionSpec as P

ALL_AXES = ("ep", "dp")
GROUP = 8
UNROLL = 8
VMEM_LIMIT = 62 << 20
LOW, HIGH = range(2)
OWN, X, Y, FAR = range(4)
COST = pl.CostEstimate(flops=20_000_000_000, bytes_accessed=20_000_000, transcendentals=0)
F32 = jnp.float32
BF16 = jnp.bfloat16


def dot(left, right, left_dim, right_dim):
    return lax.dot_general(left, right, (((left_dim,), (right_dim,)), ((), ())), preferred_element_type=F32)


def dot_nn(left, right):
    return dot(left, right, 1, 0)


def dot_nt(left, right):
    return dot(left, right, 1, 1)


def dot_tn(left, right):
    return dot(left, right, 0, 0)


def silu_parts(pre_act):
    sigma = jax.nn.sigmoid(pre_act)
    return pre_act * sigma, sigma * (1.0 + pre_act * (1.0 - sigma))


def route(meta_ref, src, first_expert, capacity, pick_ref, slot, tok_ref=None):
    top = meta_ref.shape[1] // 2
    tokens = meta_ref.shape[2]
    slots = meta_ref[src, 0:top, :].astype(jnp.int32)
    gates = meta_ref[src, top : 2 * top, :]
    expert = slots // capacity - first_expert
    row = (slots % capacity).astype(F32)
    which = lax.broadcasted_iota(jnp.int32, (GROUP, tokens), 0)
    row_of = jnp.full((GROUP, tokens), -1.0, F32)
    gate_of = jnp.zeros((GROUP, tokens), F32)
    for j in range(top):
        hit = expert[j : j + 1, :] == which
        row_of = jnp.where(hit, row[j : j + 1, :], row_of)
        gate_of = jnp.where(hit, gates[j : j + 1, :], gate_of)
    if tok_ref is not None:
        width = tok_ref.shape[1] - 4 * GROUP
        high = gate_of.astype(BF16)
        rest = gate_of - high.astype(F32)
        middle = rest.astype(BF16)
        low = (rest - middle.astype(F32)).astype(BF16)
        tok_ref[src, width : width + 4 * GROUP, :] = jnp.concatenate([high, middle, low, jnp.zeros_like(low)], axis=0)
    step = 16
    rows = lax.broadcasted_iota(jnp.int32, (step, tokens), 0).astype(F32).astype(BF16)
    for k in range(GROUP):
        wanted = jnp.broadcast_to(row_of[k : k + 1, :], (step, tokens)).astype(BF16)
        for h in range(capacity // step):
            hit = wanted == rows + jnp.asarray(h * step, BF16)
            start = k * capacity + h * step
            pick_ref[slot, src, start : start + step, :] = jnp.where(hit, jnp.asarray(1, BF16), jnp.asarray(0, BF16))


def gate_column(found, capacity):
    width = found.shape[1] - 4 * GROUP
    gates = []
    for k in range(GROUP):
        rows = found[k * capacity : (k + 1) * capacity, :]
        gates.append(rows[:, width + k : width + k + 1] + rows[:, width + GROUP + k : width + GROUP + k + 1] + rows[:, width + 2 * GROUP + k : width + 2 * GROUP + k + 1])
    return jnp.concatenate(gates, axis=0)


def schedule(groups, sources, begin, wait, dispatch, expert, combine, finish):
    group = pl.program_id(0)

    @pl.when(group == 0)
    def _():
        begin()

        def first(src, carry):
            wait(src)
            dispatch(src)
            return carry

        lax.fori_loop(0, sources, first, 0)

    @pl.when((group > 0) & (group < groups))
    def _():
        def middle(src, carry):
            combine(src)
            dispatch(src)
            return carry

        lax.fori_loop(0, sources, middle, 0)

    @pl.when(group < groups)
    def _():
        def one(k, carry):
            expert(k)
            return carry

        lax.fori_loop(0, GROUP, one, 0, unroll=UNROLL)

    @pl.when(group == groups)
    def _():
        def last(src, carry):
            finish(src)
            return carry

        lax.fori_loop(0, sources, last, 0)


def start_all(copies):
    for copy in copies:
        copy.start()


def wait_all(copies):
    for copy in copies:
        copy.wait()


def fwd_kernel(capacity, groups, base_ref, meta_ref, w1_ref, w3_ref, w2_ref, tokens_ref, out_ref, xs_ref, sum_ref, tok_ref, pick_ref, gate_ref, x_ref, o_ref, sem, out_sem, save_sem):
    group = pl.program_id(0)
    sources = tok_ref.shape[0]
    width = w1_ref.shape[1]
    now = group % 2
    before = 1 - now

    def load(src):
        return pltpu.make_async_copy(tokens_ref.at[src], tok_ref.at[src, pl.ds(0, width)], sem.at[src])

    def begin():
        for src in range(sources):
            load(src).start()

    def dispatch(src):
        route(meta_ref, src, base_ref[0] + group * GROUP, capacity, pick_ref, now, tok_ref)
        found = dot_nt(pick_ref[now, src], tok_ref[src])
        x_ref[now, src] = found.astype(BF16)
        gate_ref[src] = gate_column(found, capacity)

    def expert(k):
        here = pl.ds(pl.multiple_of(k * capacity, capacity), capacity)
        x = x_ref[now, :, here, :width].reshape(sources * capacity, width)
        ff = w1_ref.shape[2]
        a = dot_nn(x, jnp.concatenate([w1_ref[k], w3_ref[k]], axis=1))
        hidden = (jax.nn.silu(a[:, :ff]) * a[:, ff:]).astype(BF16)
        out = dot_nt(hidden, w2_ref[k]).astype(BF16).astype(F32)
        gate = gate_ref[:, here, :].reshape(sources * capacity, 1)
        o_ref[:, here, :] = (gate * out).reshape(sources, capacity, width)

    def added(src):
        rest = o_ref[src].T
        pick = pick_ref[before, src]
        parts = []
        for _ in range(3):
            parts.append(rest.astype(BF16))
            rest = rest - parts[-1].astype(F32)
        return dot_nn(parts[0], pick) + dot_nn(parts[1], pick) + dot_nn(parts[2], pick)

    def combine(src):
        @pl.when(group == 1)
        def _():
            sum_ref[src] = jnp.zeros(sum_ref.shape[1:], F32)

        sum_ref[src] += added(src)

    def store(src):
        return pltpu.make_async_copy(sum_ref.at[src], out_ref.at[src], out_sem.at[src])

    def finish(src):
        sum_ref[src] += added(src)
        store(src).start()

    def saves(step):
        slot = step % 2
        return [pltpu.make_async_copy(kept.at[slot], to.at[step], save_sem.at[slot, n]) for n, (kept, to) in enumerate(((x_ref, xs_ref),))]

    @pl.when(group >= 2)
    def _():
        wait_all(saves(group - 2))

    schedule(groups, sources, begin, lambda src: load(src).wait(), dispatch, expert, combine, finish)

    @pl.when(group < groups)
    def _():
        start_all(saves(group))

    @pl.when(group == groups)
    def _():
        wait_all(saves(group - 1))
        for src in range(sources):
            store(src).wait()


def bwd_kernel(layer, capacity, groups, held, pieces, keeps, base_ref, meta_ref, w1_ref, w3_ref, w2_ref, *refs):
    given_ref, piece_refs, other_refs, refs = refs[0], refs[1 : 1 + pieces], refs[1 + pieces : 1 + pieces + held], refs[1 + pieces + held :]
    out_ref, d1_ref, d3_ref, d2_ref, sum_ref, grad_ref, pick_ref, x_ref, g_ref, r_ref, d_ref, sem, grad_sem, out_sem, d_sem, from_ref = refs[:16]
    d_refs = (d1_ref, d3_ref, d2_ref)
    group = pl.program_id(0)
    sources = sum_ref.shape[0]
    width = w1_ref.shape[1]
    now = group % 2
    before = 1 - now
    x_slot = now if keeps else 0

    def load(src):
        return pltpu.make_async_copy(given_ref.at[src], from_ref.at[src, pl.ds(0, width)], sem.at[src])

    def loads_saved(step):
        return [pltpu.make_async_copy(given_ref.at[step], x_ref.at[step % 2], sem.at[step % 2])]

    def load_grad(src):
        piece = piece_refs[0].at[src] if pieces == 1 else piece_refs[src]
        return pltpu.make_async_copy(piece, grad_ref.at[src], grad_sem.at[src])

    def begin():
        if keeps:
            start_all(loads_saved(0))
        for src in range(sources):
            if not keeps:
                load(src).start()
            load_grad(src).start()
        if keeps:
            wait_all(loads_saved(0))

    def wait(src):
        if not keeps:
            load(src).wait()
        pltpu.make_async_copy(grad_ref.at[src], grad_ref.at[src], grad_sem.at[src]).wait()

    def dispatch(src):
        if keeps:
            route(meta_ref, src, base_ref[0] + group * GROUP, capacity, pick_ref, now)
            gate = gate_column(x_ref[now, src].astype(F32), capacity)
        else:
            route(meta_ref, src, base_ref[0] + group * GROUP, capacity, pick_ref, now, from_ref)
            found = dot_nt(pick_ref[now, src], from_ref[src])
            gate = gate_column(found, capacity)
            x_ref[0, src] = found.astype(BF16)
        g_ref[src] = (gate * dot_nt(pick_ref[now, src], grad_ref[src])).astype(BF16)

    def next_saved():
        @pl.when((group > 0) & (group < groups))
        def _():
            wait_all(loads_saved(group))

        @pl.when(group < groups - 1)
        def _():
            start_all(loads_saved(group + 1))

    def expert(k):
        here = pl.ds(pl.multiple_of(k * capacity, capacity), capacity)
        x = x_ref[x_slot, :, here, :width].reshape(sources * capacity, width)
        g = g_ref[:, here, :].reshape(sources * capacity, width)
        ff = w1_ref.shape[2]
        both = jnp.concatenate([w1_ref[k], w3_ref[k]], axis=1)
        a = dot_nn(x, both)
        a_three = a[:, ff:]
        act, slope = silu_parts(a[:, :ff])
        hidden = (act * a_three).astype(BF16)
        grad_hidden = dot_nn(g, w2_ref[k])
        grad_one = (grad_hidden * a_three * slope).astype(BF16)
        grad_three = (grad_hidden * act).astype(BF16)
        grads = jnp.concatenate([grad_one, grad_three], axis=1)
        r_ref[:, here, :] = dot_nt(grads, both).astype(BF16).reshape(sources, capacity, width)
        d13 = dot_tn(x, grads).astype(BF16)
        d2 = dot_tn(g, hidden).astype(BF16)
        for i, value in enumerate((d13[:, :ff], d13[:, ff:], d2)):
            d_ref[now, i, k] = value

    def added(src):
        return dot_tn(r_ref[src], pick_ref[before, src])

    def combine(src):
        @pl.when(group == 1)
        def _():
            sum_ref[src] = jnp.zeros(sum_ref.shape[1:], F32)

        sum_ref[src] += added(src)

    def store(src):
        return pltpu.make_async_copy(grad_ref.at[src], out_ref.at[src], out_sem.at[src])

    def finish(src):
        grad_ref[src] = (sum_ref[src] + added(src)).astype(BF16)
        store(src).start()

    def experts_at(start, step):
        return pl.ds(pl.multiple_of((start + step) * GROUP, GROUP), GROUP)

    def d_stores(step):
        slot = step % 2
        return [pltpu.make_async_copy(d_ref.at[slot, i], d_refs[i].at[layer, experts_at(base_ref[1], step)], d_sem.at[slot, i]) for i in range(3)]

    def other_load(step):
        return pltpu.make_async_copy(other_refs[0].at[:, experts_at(0, step)], refs[16].at[step % 2], refs[17].at[step % 2, 3])

    def other_stores(step):
        slot = step % 2
        return [pltpu.make_async_copy(refs[16].at[slot, i], d_refs[i].at[1 - layer, experts_at(base_ref[2], step)], refs[17].at[slot, i]) for i in range(3)]

    @pl.when(group >= 2)
    def _():
        wait_all(d_stores(group - 2))
        if held:
            wait_all(other_stores(group - 2))

    if held:
        @pl.when(group >= 1)
        def _():
            other_load(group - 1).wait()
            start_all(other_stores(group - 1))

        @pl.when(group < groups)
        def _():
            other_load(group).start()

    if keeps:
        next_saved()

    schedule(groups, sources, begin, wait, dispatch, expert, combine, finish)

    @pl.when(group < groups)
    def _():
        start_all(d_stores(group))

    @pl.when(group == groups)
    def _():
        wait_all(d_stores(group - 1))
        if held:
            wait_all(other_stores(group - 1))
        for src in range(sources):
            store(src).wait()


def weight_specs(layer, groups, width, ff):
    spec = pl.BlockSpec((None, GROUP, width, ff), lambda g, base: (layer, base[1] + jnp.minimum(g, groups - 1), 0, 0))
    return [spec, spec, spec]


def whole():
    return pl.BlockSpec(memory_space=pltpu.VMEM)


def anywhere():
    return pl.BlockSpec(memory_space=pl.ANY)


def expert_forward(layer, capacity, groups, base, tok, meta, w1, w3, w2):
    sources, width, tokens = tok.shape
    ff = w1.shape[3]
    rows = GROUP * capacity
    return pl.pallas_call(
        functools.partial(fwd_kernel, capacity, groups),
        out_shape=(
            jax.ShapeDtypeStruct((sources, width, tokens), F32),
            jax.ShapeDtypeStruct((groups, sources, rows, width + 4 * GROUP), BF16),
        ),
        grid_spec=pltpu.PrefetchScalarGridSpec(
            num_scalar_prefetch=1,
            grid=(groups + 1,),
            in_specs=[whole()] + weight_specs(layer, groups, width, ff) + [anywhere()],
            out_specs=(anywhere(),) * 2,
            scratch_shapes=[
                pltpu.VMEM((sources, width, tokens), F32),
                pltpu.VMEM((sources, width + 4 * GROUP, tokens), BF16),
                pltpu.VMEM((2, sources, rows, tokens), BF16),
                pltpu.VMEM((sources, rows, 1), F32),
                pltpu.VMEM((2, sources, rows, width + 4 * GROUP), BF16),
                pltpu.VMEM((sources, rows, width), F32),
                pltpu.SemaphoreType.DMA((sources,)),
                pltpu.SemaphoreType.DMA((sources,)),
                pltpu.SemaphoreType.DMA((2, 1)),
            ],
        ),
        compiler_params=pltpu.CompilerParams(vmem_limit_bytes=VMEM_LIMIT),
        cost_estimate=COST,
    )(base, meta, w1, w3, w2, tok)


def expert_backward(layer, capacity, groups, base, given, keeps, grads, meta, w1, w3, w2, held):
    sources, tokens = meta.shape[0], meta.shape[2]
    width = w1.shape[2]
    ff = w1.shape[3]
    rows = GROUP * capacity
    pieces = len(grads)
    grad_shape = jax.ShapeDtypeStruct(w1.shape, BF16)
    block = pltpu.VMEM((2, 3, GROUP, width, ff), BF16)
    more = [block, pltpu.SemaphoreType.DMA((2, 4))] if held else []
    return pl.pallas_call(
        functools.partial(bwd_kernel, layer, capacity, groups, len(held), pieces, keeps),
        out_shape=(jax.ShapeDtypeStruct((sources, width, tokens), BF16), grad_shape, grad_shape, grad_shape),
        grid_spec=pltpu.PrefetchScalarGridSpec(
            num_scalar_prefetch=1,
            grid=(groups + 1,),
            in_specs=[whole()] + weight_specs(layer, groups, width, ff) + [anywhere()] * (1 + pieces + len(held)),
            out_specs=(anywhere(),) * 4,
            scratch_shapes=[
                pltpu.VMEM((sources, width, tokens), F32),
                pltpu.VMEM((sources, width, tokens), BF16),
                pltpu.VMEM((2, sources, rows, tokens), BF16),
                pltpu.VMEM((2 if keeps else 1, sources, rows, width + 4 * GROUP), BF16),
                pltpu.VMEM((sources, rows, width), BF16),
                pltpu.VMEM((sources, rows, width), BF16),
                block,
                pltpu.SemaphoreType.DMA((sources,)),
                pltpu.SemaphoreType.DMA((sources,)),
                pltpu.SemaphoreType.DMA((sources,)),
                pltpu.SemaphoreType.DMA((2, 4)),
                pltpu.VMEM((8, 128), BF16) if keeps else pltpu.VMEM((sources, width + 4 * GROUP, tokens), BF16),
            ]
            + more,
        ),
        input_output_aliases={7 + pieces + i: 1 + i for i in range(len(held) - 1)},
        compiler_params=pltpu.CompilerParams(vmem_limit_bytes=VMEM_LIMIT),
        cost_estimate=COST,
    )(base, meta, w1, w3, w2, given, *grads, *held)


def place_kernel(base_ref, recv_ref, *refs):
    for i in range(3):
        refs[3 + i][...] = recv_ref[i]


def place(layer, groups, base, recv, held):
    width, ff = recv.shape[2:]
    few = 8
    spec = pl.BlockSpec((None, few, width, ff), lambda g, base: (layer, base[2] * (GROUP // few) + g, 0, 0))
    shape = jax.ShapeDtypeStruct(held[0].shape, BF16)
    return pl.pallas_call(
        place_kernel,
        out_shape=(shape, shape, shape),
        grid_spec=pltpu.PrefetchScalarGridSpec(
            num_scalar_prefetch=1,
            grid=(groups * GROUP // few,),
            in_specs=[pl.BlockSpec((3, few, width, ff), lambda g, base: (0, g, 0, 0))] + [anywhere()] * 3,
            out_specs=(spec, spec, spec),
        ),
        input_output_aliases={2: 0, 3: 1, 4: 2},
        compiler_params=pltpu.CompilerParams(vmem_limit_bytes=VMEM_LIMIT),
        cost_estimate=COST,
    )(base, recv, *held)


def neighbours():
    ep = lax.axis_index("ep")
    dp = lax.axis_index("dp")
    return ({"ep": ep + 1 - 2 * (ep % 2), "dp": dp}, {"ep": (ep + 2) % 4, "dp": dp}, {"ep": ep, "dp": 1 - dp})


def greet(devices):
    barrier = pltpu.get_barrier_semaphore()
    for device in devices:
        pl.semaphore_signal(barrier, inc=1, device_id=device, device_id_type=pl.DeviceIdType.MESH)
    pl.semaphore_wait(barrier, len(devices))


def send_block(source, target, send, recv, device):
    made = pltpu.make_async_remote_copy(src_ref=source, dst_ref=target, send_sem=send, recv_sem=recv, device_id=device, device_id_type=pl.DeviceIdType.MESH)
    made.start()
    return made


def gather_phase(devices, own_refs, out_refs, land_refs, sems, shadows):
    by_x, by_y, partner = devices
    send_sem, recv_sem, store_sem = sems
    count = len(own_refs)
    stores = []

    made = [[] for _ in own_refs]

    def copy(which, source, target, half, device):
        rows = own_refs[which].shape[0]
        span = pl.ds(0, rows) if half is None else pl.ds(half * (rows // 2), rows // 2)
        block = land_refs[which].at[source, span] if source else own_refs[which].at[span]
        n = len(made[which])
        made[which].append(send_block(block, land_refs[which].at[target, span], send_sem.at[which, n], recv_sem.at[which, n], device))
        return made[which][n]

    def store(which, slot):
        block = land_refs[which].at[slot] if slot else own_refs[which]
        started = pltpu.make_async_copy(block, out_refs[which].at[slot], store_sem.at[which, slot])
        started.start()
        stores.append(started)

    near, far, pair = [], [], []
    for which in range(count):
        near.append([copy(which, OWN, X, LOW, by_x), copy(which, OWN, Y, HIGH, by_y), copy(which, OWN, X, HIGH, by_x), copy(which, OWN, Y, LOW, by_y)])
        pair.append(copy(which, OWN, 4, None, partner))
        store(which, OWN)
    shadows[0]()
    for which in range(count):
        x_low, y_high, x_high, y_low = near[which]
        x_low.wait_recv()
        relay_low = copy(which, X, FAR, LOW, by_y)
        y_high.wait_recv()
        relay_high = copy(which, Y, FAR, HIGH, by_x)
        if not far:
            shadows[1]()
        x_high.wait_recv()
        pair_x = copy(which, X, 4 + X, None, partner)
        store(which, X)
        y_low.wait_recv()
        pair_y = copy(which, Y, 4 + Y, None, partner)
        store(which, Y)
        pair[which].wait_recv()
        store(which, 4)
        far.append((relay_low, relay_high, pair_x, pair_y))
    for which in range(count):
        relay_low, relay_high, pair_x, pair_y = far[which]
        relay_low.wait_recv()
        pair_low = copy(which, FAR, 4 + FAR, LOW, partner)
        relay_high.wait_recv()
        pair_high = copy(which, FAR, 4 + FAR, HIGH, partner)
        store(which, FAR)
        pair_x.wait_recv()
        store(which, 4 + X)
        pair_y.wait_recv()
        store(which, 4 + Y)
        pair_low.wait_recv()
        pair_high.wait_recv()
        store(which, 4 + FAR)
        for step in made[which]:
            step.wait_send()
    wait_all(stores)


def gather_scratch(*arrays):
    count = len(arrays)
    return [pltpu.VMEM((8,) + x.shape, x.dtype) for x in arrays] + [pltpu.SemaphoreType.DMA((count, n)) for n in (11, 11, 8)]


def reduce_phase(devices, part_ref, out_ref, scratch, extras, shadow):
    mine_ref, pair_ref, stage_ref, relay_ref, last_ref, send_sem, recv_sem, load_sem = scratch
    by_x, by_y, partner = devices
    rows = part_ref.shape[1]
    half = rows // 2
    low, high, full = pl.ds(0, half), pl.ds(half, half), pl.ds(0, rows)
    wire = part_ref.dtype

    made = []

    def copy(source, target, device):
        n = len(made)
        made.append(send_block(source, target, send_sem.at[n], recv_sem.at[n], device))
        return made[n]

    def chip_sum(i, span):
        return mine_ref[i, span, :].astype(F32) + pair_ref[i, span, :].astype(F32)

    loads, pair = {}, {}
    for i in (FAR, X, Y, OWN):
        loads[i] = pltpu.make_async_copy(part_ref.at[i], mine_ref.at[i], load_sem.at[i])
        loads[i].start()
        pair[i] = copy(part_ref.at[4 + i], pair_ref.at[i], partner)

    def ready(i):
        loads[i].wait()
        pair[i].wait_recv()

    ready(FAR)
    stage_ref[OWN, low, :] = chip_sum(FAR, low).astype(wire)
    relay_x = copy(stage_ref.at[OWN, low], relay_ref.at[LOW], by_x)
    stage_ref[OWN, high, :] = chip_sum(FAR, high).astype(wire)
    relay_y = copy(stage_ref.at[OWN, high], relay_ref.at[HIGH], by_y)
    ready(X)
    stage_ref[X, low, :] = chip_sum(X, low).astype(wire)
    arrive = [copy(stage_ref.at[X, low], last_ref.at[LOW, low], by_x)]
    ready(Y)
    stage_ref[Y, high, :] = chip_sum(Y, high).astype(wire)
    arrive.append(copy(stage_ref.at[Y, high], last_ref.at[HIGH, high], by_y))
    others = [copy(source, target, partner) for source, target in extras]
    relay_y.wait_recv()
    stage_ref[X, high, :] = (chip_sum(X, high) + relay_ref[HIGH].astype(F32)).astype(wire)
    arrive.append(copy(stage_ref.at[X, high], last_ref.at[LOW, high], by_x))
    relay_x.wait_recv()
    stage_ref[Y, low, :] = (chip_sum(Y, low) + relay_ref[LOW].astype(F32)).astype(wire)
    arrive.append(copy(stage_ref.at[Y, low], last_ref.at[HIGH, low], by_y))
    ready(OWN)
    out_ref[...] = chip_sum(OWN, full)
    shadow()
    for step in arrive:
        step.wait_recv()
    out_ref[...] += last_ref[LOW].astype(F32) + last_ref[HIGH].astype(F32)

    def drain():
        for step in others:
            step.wait_recv()
        for step in made:
            step.wait_send()

    return drain


def reduce_scratch(part):
    rows, tokens = part.shape[1:]
    return [
        pltpu.VMEM((4, rows, tokens), part.dtype),
        pltpu.VMEM((4, rows, tokens), part.dtype),
        pltpu.VMEM((3, rows, tokens), part.dtype),
        pltpu.VMEM((2, rows // 2, tokens), part.dtype),
        pltpu.VMEM((2, rows, tokens), part.dtype),
        pltpu.SemaphoreType.DMA((13,)),
        pltpu.SemaphoreType.DMA((13,)),
        pltpu.SemaphoreType.DMA((4,)),
    ]


def nothing():
    pass


def mix(x_ref, w_dense_ref):
    x = x_ref[...]
    return (x.astype(F32) + dot_tn(w_dense_ref[...], x)).astype(BF16)


def shared_forward(mixed, ws_gate, ws_up):
    s_one = dot_tn(ws_gate, mixed)
    s_three = dot_tn(ws_up, mixed)
    return s_one, s_three, (jax.nn.silu(s_one) * s_three).astype(BF16)


def shared_backward(grad_y, mixed, ws_gate, ws_up, ws_down, pack_ref, start):
    s_one, s_three, shared_hidden = shared_forward(mixed, ws_gate, ws_up)
    act_one, slope = silu_parts(s_one)
    grad_shared = dot_tn(ws_down, grad_y)
    grad_s_one = (grad_shared * s_three * slope).astype(BF16)
    grad_s_three = (grad_shared * act_one).astype(BF16)
    ff = ws_gate.shape[1]
    for i, value in enumerate((dot_nt(mixed, grad_s_one), dot_nt(mixed, grad_s_three), dot_nt(grad_y, shared_hidden))):
        pack_ref[:, start + i * ff : start + (i + 1) * ff] = value.astype(BF16)
    return dot_nn(ws_gate, grad_s_one) + dot_nn(ws_up, grad_s_three)


def comm_call(kernel, cid, out_shape, in_specs, out_specs, scratch, operands):
    return pl.pallas_call(
        kernel,
        out_shape=out_shape,
        in_specs=in_specs,
        out_specs=out_specs,
        scratch_shapes=scratch,
        compiler_params=pltpu.CompilerParams(collective_id=cid, has_side_effects=True, vmem_limit_bytes=VMEM_LIMIT),
        cost_estimate=COST,
    )(*operands)


def first_kernel(x_ref, w_dense_ref, meta_ref, tok_ref, metas_ref, own_ref, land_ref, land_meta_ref, *sems):
    devices = neighbours()
    own_ref[...] = mix(x_ref, w_dense_ref)
    greet(devices)
    gather_phase(devices, [own_ref, meta_ref], [tok_ref, metas_ref], [land_ref, land_meta_ref], sems, (nothing, nothing))


def first_exchange(x, w_dense, meta):
    outs = (jax.ShapeDtypeStruct((8,) + x.shape, BF16), jax.ShapeDtypeStruct((8,) + meta.shape, F32), jax.ShapeDtypeStruct(x.shape, BF16))
    return comm_call(first_kernel, 0, outs, [whole()] * 3, (anywhere(), anywhere(), whole()), gather_scratch(x, meta), (x, w_dense, meta))


def forward_kernel(part_ref, u1_ref, ws_gate_ref, ws_up_ref, ws_down_ref, w_dense_ref, tok_ref, x2_ref, u2_ref, sum_ref, shared_ref, *scratch):
    devices = neighbours()
    greet(devices)

    def shadow():
        hidden = shared_forward(u1_ref[...], ws_gate_ref[...], ws_up_ref[...])[2]
        shared_ref[...] = dot_nn(ws_down_ref[...], hidden)

    drain = reduce_phase(devices, part_ref, sum_ref, scratch[:8], [], shadow)
    x2_ref[...] = (u1_ref[...].astype(F32) + sum_ref[...] + shared_ref[...]).astype(BF16)
    u2_ref[...] = mix(x2_ref, w_dense_ref)
    gather_phase(devices, [u2_ref], [tok_ref], [scratch[8]], scratch[9:], (nothing, nothing))
    drain()


def forward_exchange(part, u1, ws_gate, ws_up, ws_down_t, w_dense):
    outs = (jax.ShapeDtypeStruct((8,) + u1.shape, BF16), jax.ShapeDtypeStruct(u1.shape, BF16), jax.ShapeDtypeStruct(u1.shape, BF16))
    scratch = [pltpu.VMEM(u1.shape, F32), pltpu.VMEM(u1.shape, F32)] + reduce_scratch(part) + gather_scratch(u1)
    specs = [anywhere()] + [whole()] * 5
    return comm_call(forward_kernel, 1, outs, specs, (anywhere(), whole(), whole()), scratch, (part, u1, ws_gate, ws_up, ws_down_t, w_dense))


def expert_half(refs, layer, target_ref):
    own = target_ref.shape[1]
    start = lax.axis_index("dp") * own
    return [(ref.at[layer, pl.ds(start, own)], target_ref.at[i]) for i, ref in enumerate(refs)]


def backward_kernel(part_ref, d1_ref, d3_ref, d2_ref, grad_y_ref, x2_ref, u2_ref, u1_ref, w_dense_ref, *refs):
    shared2, shared1, refs = refs[:3], refs[3:6], refs[6:]
    grad_all_ref, recv_ref, grad_x_ref, back_ref, pack_ref, sum_ref, mixed_ref = refs[:7]
    scratch = refs[7:]
    devices = neighbours()
    greet(devices)
    ff = shared1[0].shape[1]
    width = x2_ref.shape[0]

    def shadow():
        back_ref[...] = shared_backward(grad_y_ref[...], u2_ref[...], *(ref[...] for ref in shared2), pack_ref, 0)

    drain = reduce_phase(devices, part_ref, sum_ref, scratch[:8], expert_half((d1_ref, d3_ref, d2_ref), 1, recv_ref), shadow)
    mixed_ref[...] = (grad_y_ref[...].astype(F32) + sum_ref[...] + back_ref[...]).astype(BF16)
    grad_x_ref[...] = (mixed_ref[...].astype(F32) + dot_nn(w_dense_ref[...], mixed_ref[...])).astype(BF16)

    def dense_part():
        pack_ref[:, 6 * ff : 6 * ff + width] = dot_nt(x2_ref[...], mixed_ref[...]).astype(BF16)
        pack_ref[:, 6 * ff + width :] = jnp.zeros((width, pack_ref.shape[1] - 6 * ff - width), BF16)

    def shared_part():
        back_ref[...] = shared_backward(grad_x_ref[...], u1_ref[...], *(ref[...] for ref in shared1), pack_ref, 3 * ff)

    gather_phase(devices, [grad_x_ref], [grad_all_ref], [scratch[8]], scratch[9:], (dense_part, shared_part))
    drain()


def backward_exchange(part, held, grad_y, x2, u2, u1, w_dense, shared2, shared1):
    ff = shared1[0].shape[1]
    width = x2.shape[0]
    packed = 6 * ff + width + -(6 * ff + width) % 128
    own = held[0].shape[1] // 2
    outs = (
        jax.ShapeDtypeStruct((8,) + x2.shape, BF16),
        jax.ShapeDtypeStruct((3, own) + held[0].shape[2:], BF16),
        jax.ShapeDtypeStruct(x2.shape, BF16),
        jax.ShapeDtypeStruct(x2.shape, F32),
        jax.ShapeDtypeStruct((width, packed), BF16),
    )
    scratch = [pltpu.VMEM(x2.shape, F32), pltpu.VMEM(x2.shape, BF16)] + reduce_scratch(part) + gather_scratch(x2)
    operands = (part, *held, grad_y, x2, u2, u1, w_dense, *shared2, *shared1)
    specs = [anywhere()] * 4 + [whole()] * 11
    return comm_call(backward_kernel, 2, outs, specs, (anywhere(), anywhere()) + (whole(),) * 3, scratch, operands)


def last_kernel(part_ref, d1_ref, d3_ref, d2_ref, out_ref, recv_ref, *scratch):
    devices = neighbours()
    greet(devices)
    reduce_phase(devices, part_ref, out_ref, scratch, expert_half((d1_ref, d3_ref, d2_ref), 0, recv_ref), nothing)()


def last_exchange(part, held):
    own = held[0].shape[1] // 2
    outs = (jax.ShapeDtypeStruct(part.shape[1:], F32), jax.ShapeDtypeStruct((3, own) + held[0].shape[2:], BF16))
    return comm_call(last_kernel, 3, outs, [anywhere()] * 4, (whole(), anywhere()), reduce_scratch(part), (part, *held))


def send_over(x, flip):
    return lax.ppermute(x, "ep", [(i, i ^ flip) for i in range(4)])


def swap_cores(x):
    return lax.ppermute(x, "dp", [(0, 1), (1, 0)])


def sum_start(x):
    half = x.shape[0] // 2
    dp = lax.axis_index("dp")
    mine = lax.dynamic_slice_in_dim(x, dp * half, half, 0)
    other = lax.dynamic_slice_in_dim(x, (1 - dp) * half, half, 0)
    chip = (mine.astype(F32) + swap_cores(other).astype(F32)).astype(BF16)
    sent = [chip]
    for flip in (1, 2, 3):
        sent.append(send_over(chip, flip))
    return sent


def sum_finish(parts):
    total = sum(part.astype(F32) for part in parts).astype(BF16)
    other = swap_cores(total)
    first = lax.axis_index("dp") == 0
    return jnp.concatenate([jnp.where(first, total, other), jnp.where(first, other, total)], axis=0)


def dense_finish(grad_y, routed, shared, act, w_dense):
    grad_mixed = (grad_y.astype(F32) + routed + shared).astype(BF16)
    grad_act = (grad_mixed.astype(F32) + dot_nn(w_dense, grad_mixed)).astype(BF16)
    return grad_act, dot_nt(act, grad_mixed).astype(BF16)


def solution(mesh):
    ep_size = mesh.shape["ep"]
    dp_size = mesh.shape["dp"]
    tok_spec = P(ALL_AXES)
    route_spec = P(None, ALL_AXES)
    exp_spec = P(None, "ep")
    repl_spec = P()

    def body(act_in, grad_out, slot_ids, gate_vals, w_dense, w_gate, w_up, w_down, ws_gate, ws_up, ws_down):
        layers, local_exp = w_gate.shape[:2]
        tokens = act_in.shape[0]
        top = slot_ids.shape[2]
        own = local_exp // dp_size
        groups = own // GROUP
        capacity = 2 * tokens * top // (local_exp * ep_size)
        dp = lax.axis_index("dp")
        base = jnp.stack([lax.axis_index("ep") * local_exp + dp * own, dp * groups, (dp_size - 1 - dp) * groups]).astype(jnp.int32)
        w_down_t = jnp.swapaxes(w_down, 2, 3)
        meta = jnp.concatenate([jnp.swapaxes(slot_ids, 1, 2).astype(F32), jnp.swapaxes(gate_vals, 1, 2)], axis=1)
        meta = meta.reshape(layers * 2 * top, tokens)

        x1 = act_in.T
        grad_y2 = grad_out.T
        shared_w = [(ws_gate[layer], ws_up[layer], jnp.swapaxes(ws_down[layer], 0, 1)) for layer in range(layers)]
        tok1, metas, u1 = first_exchange(x1, w_dense[0], meta)
        tok1, grad_y2 = lax.optimization_barrier((tok1, grad_y2))
        grads2 = [grad_y2, send_over(grad_y2, 1), send_over(grad_y2, 2), send_over(grad_y2, 3)]
        grads2 = grads2 + [swap_cores(x) for x in grads2]
        meta1, meta2 = metas[:, : 2 * top], metas[:, 2 * top :]
        part, rows1 = expert_forward(0, capacity, groups, base, tok1, meta1, w_gate, w_up, w_down_t)
        tok2, x2, u2 = forward_exchange(part, u1, *shared_w[0], w_dense[1])
        back2, *held = expert_backward(1, capacity, groups, base, tok2, False, grads2, meta2, w_gate, w_up, w_down_t, [])
        grad1_all, recv2, grad_y1, shared1, early = backward_exchange(back2, held, grad_y2, x2, u2, u1, w_dense[1], shared_w[1], shared_w[0])
        ff = ws_gate.shape[2]
        width = w_dense.shape[1]
        early = sum_start(early)
        grad1_all, early[0] = lax.optimization_barrier((grad1_all, early[0]))
        back1, *held = expert_backward(0, capacity, groups, base, rows1, True, [grad1_all], meta1, w_gate, w_up, w_down_t, [recv2] + held)
        routed1, recv1 = last_exchange(back1, held)
        grad_x, g_w_dense1 = dense_finish(grad_y1, routed1, shared1, x1, w_dense[0])
        late = sum_start(g_w_dense1)
        g_gate, g_up, g_down = place(0, groups, base, recv1, held)
        g_gate, late = lax.optimization_barrier((g_gate, late))
        g_down = jnp.swapaxes(g_down, 2, 3)
        early = sum_finish(early)
        late = sum_finish(late)
        g_dense = jnp.stack([late, early[:, 6 * ff : 6 * ff + width]])
        shared = [jnp.stack([early[:, (3 + i) * ff : (4 + i) * ff], early[:, i * ff : (i + 1) * ff]]) for i in range(3)]
        return (grad_x.T, g_dense, g_gate, g_up, g_down, shared[0], shared[1], jnp.swapaxes(shared[2], 1, 2))

    return jax.shard_map(body, mesh=mesh, in_specs=(tok_spec, tok_spec, route_spec, route_spec, repl_spec, exp_spec, exp_spec, exp_spec, repl_spec, repl_spec, repl_spec), out_specs=(tok_spec, repl_spec, exp_spec, exp_spec, exp_spec, repl_spec, repl_spec, repl_spec), check_vma=False)
```

time: 506 us -> 479 us (0.947)
  matrix products: 21.7 us -> 1.91 us
  Pallas kernels: 432 us -> 423 us
    dot_general x23 -> x2, matrix products: 21.7 us -> 1.91 us  [dot(): lax.dot_general(left, right, (((left_dim,), (right_dim,)), ((), ())), pre...]
    pallas_call x2, Pallas kernels: 138 us -> 129 us  [expert_backward(): pl.pallas_call(functools.partial(bwd_kernel, layer, capacity, groups, len...]
    pallas_call x6 -> x4, Pallas kernels: 207 us -> 206 us  [comm_call(): pl.pallas_call(kernel, out_shape=out_shape, in_specs=in_specs, out_specs=...]
  transfers between devices with their start and end apart: 17 -> 17, of which waited for: 4 -> 5; matrix products, arithmetic and copies ran while one was open for 4% -> 2% of each run, Pallas kernels for 39% -> 35%
where the time goes in v1:
time: 479 us
  Pallas kernels  423 us (88%)
  waiting for transfers between devices  22.5 us (5%)
  starting transfers between devices  11.6 us (2%)
  other arithmetic  10.3 us (2%)
  local copies, waits for them, and re-layouts  8.7 us (2%)
    pallas_call x4, Pallas kernels, comm_call(): pl.pallas_call(kernel, out_shape=out_shape, in_specs=in_specs, out_specs=...  206 us
    pallas_call x2, Pallas kernels, expert_backward(): pl.pallas_call(functools.partial(bwd_kernel, layer, capacity, groups, len...  129 us
    pallas_call x1, Pallas kernels, expert_forward(): pl.pallas_call(functools.partial(fwd_kernel, capacity, groups), out_shape...  74 us
    ppermute x9, waiting for transfers between devices, send_over(): return lax.ppermute(x, 'ep', [(i, i ^ flip) for i in range(4)])  19.4 us
    pallas_call x1, Pallas kernels, place(): pl.pallas_call(place_kernel, out_shape=(shape, shape, shape), grid_spec=p...  13.2 us
  transfers between devices with their start and end apart: 17, of which 5 were waited for; matrix products, arithmetic and copies ran while one was open for 2% of the time, Pallas kernels for 35%

profile of v1, /device:TPU:0, one launch (start us, length us, event | category | flops | bytes accessed | tf_op | source)
XLA Modules:
  0.0 478.6 jit_solution(13551988818288667975)
XLA Ops:
  0.6 0.8 convert_bitcast_fusion
  1.5 2.1 slice_bitcast_fusion
  3.6 0.6 pad_maximum_fusion.4
  4.2 36.9 %shard_map.170 = (bf16[8,448,768]{2,1,0:T(8,128)(2,1)}, f32[8,32,768]{2,1,0:T(8,128)}, bf16[448,768]{1,0:T(8,128)(2,1)}) custom-call(bf16[448,768]{1,0:T(8,128)(2,1)} %bitcast.81, bf16[448,448]{1,0:T(8,128)(2,1)} %get-tuple-element.87.w_dense_ref, f32[32,768]{1,0:T(8,128)} %bitcast.79), custom_call_target="tpu_custom_call" | custom-call | flops 20000000000 | bytes 20000000 | tf_op jit(solution)/shard_map/pallas_call | solution.py:647
  41.2 0.1 collective-permute-start.3
  41.3 1.5 collective-permute-start.2
  42.8 1.0 collective-permute-start.1
  43.7 1.1 collective-permute-start
  44.8 2.1 fusion.17
  46.9 0.7 pad_add_fusion.base_ref
  47.5 74.0 %shard_map.171 = (f32[8,448,768]{2,1,0:T(8,128)}, bf16[6,8,256,480]{3,2,1,0:T(8,128)(2,1)}) custom-call(s32[3]{0:T(128)} %pad_add_fusion.base_ref, f32[8,16,768]{2,1,0:T(8,128)} %get-tuple-element.88.meta_ref, bf16[2,96,448,128]{3,2,1,0:T(8,128)(2,1)} %w1_ref.5, bf16[2,96,448,128]{3,2,1,0:T(8,128)(2,1)} %w3_ref.5, bf16[2,96,448,128]{3,2,1,0:T(8,128)(2,1)} %bitcast.70, ...), custom_call_target="tpu_custom_call" | custom-call | flops 20000000000 | bytes 20000000 | tf_op jit(solution)/shard_map/pallas_call | solution.py:363
  121.5 1.7 slice_bitcast_fusion.2
  123.2 0.8 slice_bitcast_fusion.3
  124.0 0.5 collective-permute-start.5
  124.5 79.5 %shard_map.172 = (bf16[8,448,768]{2,1,0:T(8,128)(2,1)}, bf16[448,768]{1,0:T(8,128)(2,1)}, bf16[448,768]{1,0:T(8,128)(2,1)}) custom-call(f32[8,448,768]{2,1,0:T(8,128)} %get-tuple-element.46.part_ref, bf16[448,768]{1,0:T(8,128)(2,1)} %get-tuple-element.47.u1_ref, bf16[448,128]{1,0:T(8,128)(2,1)} %get-tuple-element.98.ws_gate_ref.refs_3_, ...), custom_call_target="tpu_custom_call" | custom-call | flops 20000000000 | bytes 20000000 | tf_op jit(solution)/shard_map/pallas_call | solution.py:647
  204.1 0.8 copy-done.6
  204.9 67.9 %shard_map.173 = (bf16[8,448,768]{2,1,0:T(8,128)(2,1)}, bf16[2,96,448,128]{3,2,1,0:T(8,128)(2,1)}, bf16[2,96,448,128]{3,2,1,0:T(8,128)(2,1)}, bf16[2,96,448,128]{3,2,1,0:T(8,128)(2,1)}) custom-call(s32[3]{0:T(128)} %pad_add_fusion.base_ref, f32[8,16,768]{2,1,0:T(8,128)} %get-tuple-element.89.meta_ref, bf16[2,96,448,128]{3,2,1,0:T(8,128)(2,1)} %w1_ref.5, ...), custom_call_target="tpu_custom_call" | custom-call | flops 20000000000 | bytes 20000000 | tf_op jit(solution)/shard_map/pallas_call | solution.py:400
  272.8 57.5 %shard_map.174 = (bf16[8,448,768]{2,1,0:T(8,128)(2,1)}, bf16[3,48,448,128]{3,2,1,0:T(8,128)(2,1)}, bf16[448,768]{1,0:T(8,128)(2,1)}, f32[448,768]{1,0:T(8,128)}, bf16[448,1280]{1,0:T(8,128)(2,1)}) custom-call(bf16[8,448,768]{2,1,0:T(8,128)(2,1)} %get-tuple-element.50.part_ref, bf16[2,96,448,128]{3,2,1,0:T(8,128)(2,1)} %get-tuple-element.51.d1_ref.refs_3_, ...), custom_call_target="tpu_custom_call" | custom-call | flops 20000000000 | bytes 20000000 | tf_op jit(solution)/shard_map/pallas_call | solution.py:647
  330.3 1.2 constant_dynamic-slice_fusion
  331.5 1.3 collective-permute-start.7
  332.8 1.6 collective-permute-done.7
  334.4 0.1 add_convert_fusion.2
  334.6 61.4 %shard_map.175 = (bf16[8,448,768]{2,1,0:T(8,128)(2,1)}, bf16[2,96,448,128]{3,2,1,0:T(8,128)(2,1)}, bf16[2,96,448,128]{3,2,1,0:T(8,128)(2,1)}, bf16[2,96,448,128]{3,2,1,0:T(8,128)(2,1)}) custom-call(s32[3]{0:T(128)} %pad_add_fusion.base_ref, f32[8,16,768]{2,1,0:T(8,128)} %get-tuple-element.88.meta_ref, ...), custom_call_target="tpu_custom_call", output_to_operand_aliasing={{1}: (8, {}), {2}: (9, {}), {3}: (10, {})} | custom-call | flops 20000000000 | bytes 20000000 | tf_op jit(solution)/shard_map/pallas_call | solution.py:400
  396.0 32.2 %shard_map.176 = (f32[448,768]{1,0:T(8,128)}, bf16[3,48,448,128]{3,2,1,0:T(8,128)(2,1)}) custom-call(bf16[8,448,768]{2,1,0:T(8,128)(2,1)} %get-tuple-element.62.part_ref, bf16[2,96,448,128]{3,2,1,0:T(8,128)(2,1)} %get-tuple-element.63.d1_ref.refs_0_, bf16[2,96,448,128]{3,2,1,0:T(8,128)(2,1)} %get-tuple-element.64.d3_ref.refs_1_, ...), custom_call_target="tpu_custom_call" | custom-call | flops 20000000000 | bytes 20000000 | tf_op jit(solution)/shard_map/pallas_call | solution.py:647
  428.2 1.8 add_convert_fusion
  430.1 0.5 convolution_convert_fusion
  430.6 0.1 collective-permute-start.8
  430.8 1.4 collective-permute-done.8
  432.2 1.5 collective-permute-start.11
  433.7 1.5 collective-permute-start.15
  435.2 0.4 collective-permute-start.14
  435.5 1.6 collective-permute-start.13
  437.2 0.3 collective-permute-start.10
  437.5 4.3 collective-permute-done.11
  441.8 0.3 collective-permute-start.9
  442.1 13.2 %shard_map.177 = (bf16[2,96,448,128]{3,2,1,0:T(8,128)(2,1)}, bf16[2,96,448,128]{3,2,1,0:T(8,128)(2,1)}, bf16[2,96,448,128]{3,2,1,0:T(8,128)(2,1)}) custom-call(s32[3]{0:T(128)} %pad_add_fusion.base_ref, bf16[3,48,448,128]{3,2,1,0:T(8,128)(2,1)} %get-tuple-element.68.recv_ref, ...), custom_call_target="tpu_custom_call", output_to_operand_aliasing={{0}: (2, {}), {1}: (3, {}), {2}: (4, {})} | custom-call | flops 20000000000 | bytes 20000000 | tf_op jit(solution)/shard_map/pallas_call | solution.py:440
  455.3 15.1 %collective-permute-done.10 = bf16[224,448]{1,0:T(8,128)(2,1)} collective-permute-done((bf16[224,448]{1,0:T(8,128)(2,1)S(1)}, bf16[224,448]{1,0:T(8,128)(2,1)}, u32[]{:S(2)}, u32[]{:S(2)}) %collective-permute-start.10) | collective-permute-done | bytes 200736 | tf_op jit(solution)/shard_map/ppermute | solution.py:756
  470.4 1.3 add_convert_fusion.3
  471.8 1.4 add_convert_fusion.1
  473.2 0.4 collective-permute-start.16
  473.6 1.4 fusion.2
  475.1 0.1 collective-permute-done.16
  475.2 0.1 broadcast_select_fusion
  475.3 0.1 fusion.16
  475.5 0.7 maximum_bitcast_fusion.1
  476.2 0.7 pad_maximum_fusion.1
  476.9 0.7 pad_maximum_fusion.2
  477.6 1.0 pad_maximum_fusion
  (41 shorter events, 0.4 us)
Async XLA Ops:
  0.6 3.0 copy-start.9
  4.2 36.9 %copy-start = (bf16[768,448]{0,1:T(8,128)(2,1)S(1)}, bf16[768,448]{0,1:T(8,128)(2,1)}, u32[]{:S(2)}) copy-start(bf16[768,448]{0,1:T(8,128)(2,1)} %param.12) | copy-start | bytes 2064388
  41.2 162.9 %collective-permute-start.3 = (bf16[448,768]{1,0:T(8,128)(2,1)S(1)}, bf16[448,768]{1,0:T(8,128)(2,1)S(1)}, u32[]{:S(2)}, u32[]{:S(2)}) collective-permute-start(bf16[448,768]{1,0:T(8,128)(2,1)S(1)} %bitcast.75), channel_id=1, source_target_pairs={{0,1},{1,0},{2,3},{3,2},{4,5},{5,4},{6,7},{7,6}} | collective-permute-start | bytes 2064392 | tf_op jit(solution)/shard_map/ppermute | solution.py:760
  41.3 82.6 %collective-permute-start.2 = (bf16[448,768]{1,0:T(8,128)(2,1)S(1)}, bf16[448,768]{1,0:T(8,128)(2,1)}, u32[]{:S(2)}, u32[]{:S(2)}) collective-permute-start(bf16[448,768]{1,0:T(8,128)(2,1)S(1)} %bitcast.76), channel_id=1, source_target_pairs={{0,6},{2,4},{4,2},{6,0},{1,7},{3,5},{5,3},{7,1}} | collective-permute-start | bytes 2064392 | tf_op jit(solution)/shard_map/ppermute | solution.py:756
  42.8 81.2 %collective-permute-start.1 = (bf16[448,768]{1,0:T(8,128)(2,1)S(1)}, bf16[448,768]{1,0:T(8,128)(2,1)}, u32[]{:S(2)}, u32[]{:S(2)}) collective-permute-start(bf16[448,768]{1,0:T(8,128)(2,1)S(1)} %bitcast.77), channel_id=1, source_target_pairs={{0,4},{2,6},{4,0},{6,2},{1,5},{3,7},{5,1},{7,3}} | collective-permute-start | bytes 2064392 | tf_op jit(solution)/shard_map/ppermute | solution.py:756
  43.7 80.7 %collective-permute-start = (bf16[448,768]{1,0:T(8,128)(2,1)S(1)}, bf16[448,768]{1,0:T(8,128)(2,1)}, u32[]{:S(2)}, u32[]{:S(2)}) collective-permute-start(bf16[448,768]{1,0:T(8,128)(2,1)S(1)} %bitcast.78), channel_id=1, source_target_pairs={{0,2},{2,0},{4,6},{6,4},{1,3},{3,1},{5,7},{7,5}} | collective-permute-start | bytes 2064392 | tf_op jit(solution)/shard_map/ppermute | solution.py:756
  47.5 75.7 %copy-start.7 = (bf16[2,448,128]{2,1,0:T(8,128)(2,1)S(1)}, bf16[2,448,128]{2,1,0:T(8,128)(2,1)}, u32[]{:S(2)}) copy-start(bf16[2,448,128]{2,1,0:T(8,128)(2,1)} %param.20) | copy-start | bytes 688132
  47.5 75.7 %copy-start.8 = (bf16[2,448,128]{2,1,0:T(8,128)(2,1)S(1)}, bf16[2,448,128]{2,1,0:T(8,128)(2,1)}, u32[]{:S(2)}) copy-start(bf16[2,448,128]{2,1,0:T(8,128)(2,1)} %param.19) | copy-start | bytes 688132
  124.0 80.1 %collective-permute-start.6 = (bf16[448,768]{1,0:T(8,128)(2,1)}, bf16[448,768]{1,0:T(8,128)(2,1)}, u32[]{:S(2)}, u32[]{:S(2)}) collective-permute-start(bf16[448,768]{1,0:T(8,128)(2,1)} %collective-permute-done.2.refs_4_), channel_id=1, source_target_pairs={{0,1},{1,0},{2,3},{3,2},{4,5},{5,4},{6,7},{7,6}} | collective-permute-start | bytes 2064392 | tf_op jit(solution)/shard_map/ppermute | solution.py:760
  124.0 80.1 %collective-permute-start.5 = (bf16[448,768]{1,0:T(8,128)(2,1)}, bf16[448,768]{1,0:T(8,128)(2,1)}, u32[]{:S(2)}, u32[]{:S(2)}) collective-permute-start(bf16[448,768]{1,0:T(8,128)(2,1)} %collective-permute-done.1.refs_3_), channel_id=1, source_target_pairs={{0,1},{1,0},{2,3},{3,2},{4,5},{5,4},{6,7},{7,6}} | collective-permute-start | bytes 2064392 | tf_op jit(solution)/shard_map/ppermute | solution.py:760
  124.5 79.6 %collective-permute-start.4 = (bf16[448,768]{1,0:T(8,128)(2,1)}, bf16[448,768]{1,0:T(8,128)(2,1)}, u32[]{:S(2)}, u32[]{:S(2)}) collective-permute-start(bf16[448,768]{1,0:T(8,128)(2,1)} %collective-permute-done.refs_2_), channel_id=1, source_target_pairs={{0,1},{1,0},{2,3},{3,2},{4,5},{5,4},{6,7},{7,6}} | collective-permute-start | bytes 2064392 | tf_op jit(solution)/shard_map/ppermute | solution.py:760
  204.1 0.8 copy-start.6
  330.3 4.1 copy-start.2
  331.5 2.9 collective-permute-start.7
  396.0 32.2 %copy-start.1 = (f32[448,768]{1,0:T(8,128)S(1)}, f32[448,768]{1,0:T(8,128)}, u32[]{:S(2)}) copy-start(f32[448,768]{1,0:T(8,128)} %get-tuple-element.67) | copy-start | bytes 4128772
  428.2 1.8 copy-start.10
  430.0 2.2 copy-start.4
  430.6 1.5 collective-permute-start.8
  432.2 9.6 %collective-permute-start.11 = (bf16[224,448]{1,0:T(8,128)(2,1)S(1)}, bf16[224,448]{1,0:T(8,128)(2,1)}, u32[]{:S(2)}, u32[]{:S(2)}) collective-permute-start(bf16[224,448]{1,0:T(8,128)(2,1)S(1)} %fusion.5), channel_id=1, source_target_pairs={{0,6},{2,4},{4,2},{6,0},{1,7},{3,5},{5,3},{7,1}} | collective-permute-start | bytes 602120 | tf_op jit(solution)/shard_map/ppermute | solution.py:756
  433.7 38.0 %collective-permute-start.15 = (bf16[224,1280]{1,0:T(8,128)(2,1)S(1)}, bf16[224,1280]{1,0:T(8,128)(2,1)S(1)}, u32[]{:S(2)}, u32[]{:S(2)}) collective-permute-start(bf16[224,1280]{1,0:T(8,128)(2,1)S(1)} %add_convert_fusion.2), channel_id=1, source_target_pairs={{0,6},{2,4},{4,2},{6,0},{1,7},{3,5},{5,3},{7,1}} | collective-permute-start | bytes 1720328 | tf_op jit(solution)/shard_map/ppermute | solution.py:756
  435.2 36.6 %collective-permute-start.14 = (bf16[224,1280]{1,0:T(8,128)(2,1)S(1)}, bf16[224,1280]{1,0:T(8,128)(2,1)S(1)}, u32[]{:S(2)}, u32[]{:S(2)}) collective-permute-start(bf16[224,1280]{1,0:T(8,128)(2,1)S(1)} %add_convert_fusion.2), channel_id=1, source_target_pairs={{0,4},{2,6},{4,0},{6,2},{1,5},{3,7},{5,1},{7,3}} | collective-permute-start | bytes 1720328 | tf_op jit(solution)/shard_map/ppermute | solution.py:756
  435.5 36.2 %collective-permute-start.13 = (bf16[224,1280]{1,0:T(8,128)(2,1)S(1)}, bf16[224,1280]{1,0:T(8,128)(2,1)}, u32[]{:S(2)}, u32[]{:S(2)}) collective-permute-start(bf16[224,1280]{1,0:T(8,128)(2,1)S(1)} %add_convert_fusion.2), channel_id=1, source_target_pairs={{0,2},{2,0},{4,6},{6,4},{1,3},{3,1},{5,7},{7,5}} | collective-permute-start | bytes 1720328 | tf_op jit(solution)/shard_map/ppermute | solution.py:756
  437.2 33.2 %collective-permute-start.10 = (bf16[224,448]{1,0:T(8,128)(2,1)S(1)}, bf16[224,448]{1,0:T(8,128)(2,1)}, u32[]{:S(2)}, u32[]{:S(2)}) collective-permute-start(bf16[224,448]{1,0:T(8,128)(2,1)S(1)} %fusion.5), channel_id=1, source_target_pairs={{0,4},{2,6},{4,0},{6,2},{1,5},{3,7},{5,1},{7,3}} | collective-permute-start | bytes 602120 | tf_op jit(solution)/shard_map/ppermute | solution.py:756
  441.8 28.6 %collective-permute-start.9 = (bf16[224,448]{1,0:T(8,128)(2,1)S(1)}, bf16[224,448]{1,0:T(8,128)(2,1)}, u32[]{:S(2)}, u32[]{:S(2)}) collective-permute-start(bf16[224,448]{1,0:T(8,128)(2,1)S(1)} %fusion.5), channel_id=1, source_target_pairs={{0,2},{2,0},{4,6},{6,4},{1,3},{3,1},{5,7},{7,5}} | collective-permute-start | bytes 602120 | tf_op jit(solution)/shard_map/ppermute | solution.py:756
  471.7 1.9 copy-start.3
  471.7 1.9 copy-start.5
  471.7 3.3 collective-permute-start.12
  473.2 2.0 collective-permute-start.16

commit v2 on v1

--- a/solution.py
+++ b/solution.py
@@ -38,11 +38,12 @@
     return pre_act * sigma, sigma * (1.0 + pre_act * (1.0 - sigma))
 
 
-def route(meta_ref, src, first_expert, capacity, pick_ref, slot, tok_ref=None):
-    top = meta_ref.shape[1] // 2
+def route(meta_ref, layer, src, first_expert, capacity, pick_ref, slot, tok_ref=None):
+    top = meta_ref.shape[1] // 4
     tokens = meta_ref.shape[2]
-    slots = meta_ref[src, 0:top, :].astype(jnp.int32)
-    gates = meta_ref[src, top : 2 * top, :]
+    start = 2 * layer * top
+    slots = meta_ref[src, start : start + top, :].astype(jnp.int32)
+    gates = meta_ref[src, start + top : start + 2 * top, :]
     expert = slots // capacity - first_expert
     row = (slots % capacity).astype(F32)
     which = lax.broadcasted_iota(jnp.int32, (GROUP, tokens), 0)
@@ -128,7 +129,7 @@
         copy.wait()
 
 
-def fwd_kernel(capacity, groups, base_ref, meta_ref, w1_ref, w3_ref, w2_ref, tokens_ref, out_ref, xs_ref, sum_ref, tok_ref, pick_ref, gate_ref, x_ref, o_ref, sem, out_sem, save_sem):
+def fwd_kernel(layer, capacity, groups, base_ref, meta_ref, w1_ref, w3_ref, w2_ref, tokens_ref, out_ref, xs_ref, sum_ref, tok_ref, pick_ref, gate_ref, x_ref, o_ref, sem, out_sem, save_sem):
     group = pl.program_id(0)
     sources = tok_ref.shape[0]
     width = w1_ref.shape[1]
@@ -143,7 +144,7 @@
             load(src).start()
 
     def dispatch(src):
-        route(meta_ref, src, base_ref[0] + group * GROUP, capacity, pick_ref, now, tok_ref)
+        route(meta_ref, layer, src, base_ref[0] + group * GROUP, capacity, pick_ref, now, tok_ref)
         found = dot_nt(pick_ref[now, src], tok_ref[src])
         x_ref[now, src] = found.astype(BF16)
         gate_ref[src] = gate_column(found, capacity)
@@ -240,10 +241,10 @@
 
     def dispatch(src):
         if keeps:
-            route(meta_ref, src, base_ref[0] + group * GROUP, capacity, pick_ref, now)
+            route(meta_ref, layer, src, base_ref[0] + group * GROUP, capacity, pick_ref, now)
             gate = gate_column(x_ref[now, src].astype(F32), capacity)
         else:
-            route(meta_ref, src, base_ref[0] + group * GROUP, capacity, pick_ref, now, from_ref)
+            route(meta_ref, layer, src, base_ref[0] + group * GROUP, capacity, pick_ref, now, from_ref)
             found = dot_nt(pick_ref[now, src], from_ref[src])
             gate = gate_column(found, capacity)
             x_ref[0, src] = found.astype(BF16)
@@ -361,7 +362,7 @@
     ff = w1.shape[3]
     rows = GROUP * capacity
     return pl.pallas_call(
-        functools.partial(fwd_kernel, capacity, groups),
+        functools.partial(fwd_kernel, layer, capacity, groups),
         out_shape=(
             jax.ShapeDtypeStruct((sources, width, tokens), F32),
             jax.ShapeDtypeStruct((groups, sources, rows, width + 4 * GROUP), BF16),
@@ -520,6 +521,8 @@
         relay_low, relay_high, pair_x, pair_y = far[which]
         relay_low.wait_recv()
         pair_low = copy(which, FAR, 4 + FAR, LOW, partner)
+        if which == 0:
+            shadows[2]()
         relay_high.wait_recv()
         pair_high = copy(which, FAR, 4 + FAR, HIGH, partner)
         store(which, FAR)
@@ -620,9 +623,9 @@
     pass
 
 
-def mix(x_ref, w_dense_ref):
+def mix(x_ref, w_dense):
     x = x_ref[...]
-    return (x.astype(F32) + dot_tn(w_dense_ref[...], x)).astype(BF16)
+    return (x.astype(F32) + dot_tn(w_dense, x)).astype(BF16)
 
 
 def shared_forward(mixed, ws_gate, ws_up):
@@ -657,9 +660,9 @@
 
 def first_kernel(x_ref, w_dense_ref, meta_ref, tok_ref, metas_ref, own_ref, land_ref, land_meta_ref, *sems):
     devices = neighbours()
-    own_ref[...] = mix(x_ref, w_dense_ref)
+    own_ref[...] = mix(x_ref, w_dense_ref[0])
     greet(devices)
-    gather_phase(devices, [own_ref, meta_ref], [tok_ref, metas_ref], [land_ref, land_meta_ref], sems, (nothing, nothing))
+    gather_phase(devices, [own_ref, meta_ref], [tok_ref, metas_ref], [land_ref, land_meta_ref], sems, (nothing,) * 3)
 
 
 def first_exchange(x, w_dense, meta):
@@ -672,13 +675,13 @@
     greet(devices)
 
     def shadow():
-        hidden = shared_forward(u1_ref[...], ws_gate_ref[...], ws_up_ref[...])[2]
-        shared_ref[...] = dot_nn(ws_down_ref[...], hidden)
+        hidden = shared_forward(u1_ref[...], ws_gate_ref[0], ws_up_ref[0])[2]
+        shared_ref[...] = dot_nn(ws_down_ref[0], hidden)
 
     drain = reduce_phase(devices, part_ref, sum_ref, scratch[:8], [], shadow)
     x2_ref[...] = (u1_ref[...].astype(F32) + sum_ref[...] + shared_ref[...]).astype(BF16)
-    u2_ref[...] = mix(x2_ref, w_dense_ref)
-    gather_phase(devices, [u2_ref], [tok_ref], [scratch[8]], scratch[9:], (nothing, nothing))
+    u2_ref[...] = mix(x2_ref, w_dense_ref[1])
+    gather_phase(devices, [u2_ref], [tok_ref], [scratch[8]], scratch[9:], (nothing,) * 3)
     drain()
 
 
@@ -695,35 +698,57 @@
     return [(ref.at[layer, pl.ds(start, own)], target_ref.at[i]) for i, ref in enumerate(refs)]
 
 
-def backward_kernel(part_ref, d1_ref, d3_ref, d2_ref, grad_y_ref, x2_ref, u2_ref, u1_ref, w_dense_ref, *refs):
-    shared2, shared1, refs = refs[:3], refs[3:6], refs[6:]
-    grad_all_ref, recv_ref, grad_x_ref, back_ref, pack_ref, sum_ref, mixed_ref = refs[:7]
-    scratch = refs[7:]
+def pair_half(partner, pack_ref, land_ref, sems):
+    half = land_ref.shape[0]
+    dp = lax.axis_index("dp")
+    sent = []
+
+    def start():
+        theirs = pack_ref.at[pl.ds(pl.multiple_of((1 - dp) * half, 16), half)]
+        sent.append(send_block(theirs, land_ref, sems.at[0], sems.at[1], partner))
+
+    def finish():
+        sent[0].wait()
+        mine = pack_ref[pl.ds(pl.multiple_of(dp * half, 16), half), :]
+        return (mine.astype(F32) + land_ref[...].astype(F32)).astype(BF16)
+
+    return start, finish
+
+
+def pair_scratch(shape):
+    return [pltpu.VMEM(shape, BF16), pltpu.VMEM((shape[0] // 2, shape[1]), BF16), pltpu.SemaphoreType.DMA((2,))]
+
+
+def backward_kernel(part_ref, d1_ref, d3_ref, d2_ref, grad_y_ref, x2_ref, u2_ref, u1_ref, w_dense_ref, ws_gate_ref, ws_up_ref, ws_down_ref, *refs):
+    grad_all_ref, recv_ref, grad_x_ref, back_ref, chip_ref, sum_ref, mixed_ref, pack_ref, land_ref, pair_sem = refs[:10]
+    scratch = refs[10:]
     devices = neighbours()
     greet(devices)
-    ff = shared1[0].shape[1]
+    ff = ws_gate_ref.shape[2]
     width = x2_ref.shape[0]
+    start_pair, finish_pair = pair_half(devices[2], pack_ref, land_ref, pair_sem)
 
     def shadow():
-        back_ref[...] = shared_backward(grad_y_ref[...], u2_ref[...], *(ref[...] for ref in shared2), pack_ref, 0)
+        back_ref[...] = shared_backward(grad_y_ref[...], u2_ref[...], ws_gate_ref[1], ws_up_ref[1], ws_down_ref[1], pack_ref, 0)
 
     drain = reduce_phase(devices, part_ref, sum_ref, scratch[:8], expert_half((d1_ref, d3_ref, d2_ref), 1, recv_ref), shadow)
     mixed_ref[...] = (grad_y_ref[...].astype(F32) + sum_ref[...] + back_ref[...]).astype(BF16)
-    grad_x_ref[...] = (mixed_ref[...].astype(F32) + dot_nn(w_dense_ref[...], mixed_ref[...])).astype(BF16)
+    grad_x_ref[...] = (mixed_ref[...].astype(F32) + dot_nn(w_dense_ref[1], mixed_ref[...])).astype(BF16)
 
     def dense_part():
         pack_ref[:, 6 * ff : 6 * ff + width] = dot_nt(x2_ref[...], mixed_ref[...]).astype(BF16)
         pack_ref[:, 6 * ff + width :] = jnp.zeros((width, pack_ref.shape[1] - 6 * ff - width), BF16)
 
     def shared_part():
-        back_ref[...] = shared_backward(grad_x_ref[...], u1_ref[...], *(ref[...] for ref in shared1), pack_ref, 3 * ff)
-
-    gather_phase(devices, [grad_x_ref], [grad_all_ref], [scratch[8]], scratch[9:], (dense_part, shared_part))
+        back_ref[...] = shared_backward(grad_x_ref[...], u1_ref[...], ws_gate_ref[0], ws_up_ref[0], ws_down_ref[0], pack_ref, 3 * ff)
+
+    gather_phase(devices, [grad_x_ref], [grad_all_ref], [scratch[8]], scratch[9:], (dense_part, shared_part, start_pair))
+    chip_ref[...] = finish_pair()
     drain()
 
 
-def backward_exchange(part, held, grad_y, x2, u2, u1, w_dense, shared2, shared1):
-    ff = shared1[0].shape[1]
+def backward_exchange(part, held, grad_y, x2, u2, u1, w_dense, ws_gate, ws_up, ws_down_t):
+    ff = ws_gate.shape[2]
     width = x2.shape[0]
     packed = 6 * ff + width + -(6 * ff + width) % 128
     own = held[0].shape[1] // 2
@@ -732,24 +757,34 @@
         jax.ShapeDtypeStruct((3, own) + held[0].shape[2:], BF16),
         jax.ShapeDtypeStruct(x2.shape, BF16),
         jax.ShapeDtypeStruct(x2.shape, F32),
-        jax.ShapeDtypeStruct((width, packed), BF16),
+        jax.ShapeDtypeStruct((width // 2, packed), BF16),
     )
-    scratch = [pltpu.VMEM(x2.shape, F32), pltpu.VMEM(x2.shape, BF16)] + reduce_scratch(part) + gather_scratch(x2)
-    operands = (part, *held, grad_y, x2, u2, u1, w_dense, *shared2, *shared1)
-    specs = [anywhere()] * 4 + [whole()] * 11
+    scratch = [pltpu.VMEM(x2.shape, F32), pltpu.VMEM(x2.shape, BF16)] + pair_scratch((width, packed)) + reduce_scratch(part) + gather_scratch(x2)
+    operands = (part, *held, grad_y, x2, u2, u1, w_dense, ws_gate, ws_up, ws_down_t)
+    specs = [anywhere()] * 4 + [whole()] * 8
     return comm_call(backward_kernel, 2, outs, specs, (anywhere(), anywhere()) + (whole(),) * 3, scratch, operands)
 
 
-def last_kernel(part_ref, d1_ref, d3_ref, d2_ref, out_ref, recv_ref, *scratch):
+def last_kernel(part_ref, d1_ref, d3_ref, d2_ref, grad_y_ref, back_ref, x_ref, w_dense_ref, grad_x_ref, recv_ref, chip_ref, sum_ref, mixed_ref, pack_ref, land_ref, pair_sem, *scratch):
     devices = neighbours()
     greet(devices)
-    reduce_phase(devices, part_ref, out_ref, scratch, expert_half((d1_ref, d3_ref, d2_ref), 0, recv_ref), nothing)()
-
-
-def last_exchange(part, held):
+    start_pair, finish_pair = pair_half(devices[2], pack_ref, land_ref, pair_sem)
+    drain = reduce_phase(devices, part_ref, sum_ref, scratch, expert_half((d1_ref, d3_ref, d2_ref), 0, recv_ref), nothing)
+    mixed_ref[...] = (grad_y_ref[...].astype(F32) + sum_ref[...] + back_ref[...]).astype(BF16)
+    pack_ref[...] = dot_nt(x_ref[...], mixed_ref[...]).astype(BF16)
+    grad_x_ref[...] = (mixed_ref[...].astype(F32) + dot_nn(w_dense_ref[0], mixed_ref[...])).astype(BF16)
+    start_pair()
+    drain()
+    chip_ref[...] = finish_pair()
+
+
+def last_exchange(part, held, grad_y, back, x, w_dense):
     own = held[0].shape[1] // 2
-    outs = (jax.ShapeDtypeStruct(part.shape[1:], F32), jax.ShapeDtypeStruct((3, own) + held[0].shape[2:], BF16))
-    return comm_call(last_kernel, 3, outs, [anywhere()] * 4, (whole(), anywhere()), reduce_scratch(part), (part, *held))
+    width = x.shape[0]
+    outs = (jax.ShapeDtypeStruct(x.shape, BF16), jax.ShapeDtypeStruct((3, own) + held[0].shape[2:], BF16), jax.ShapeDtypeStruct((width // 2, width), BF16))
+    scratch = [pltpu.VMEM(x.shape, F32), pltpu.VMEM(x.shape, BF16)] + pair_scratch((width, width)) + reduce_scratch(part)
+    specs = [anywhere()] * 4 + [whole()] * 4
+    return comm_call(last_kernel, 3, outs, specs, (whole(), anywhere(), whole()), scratch, (part, *held, grad_y, back, x, w_dense))
 
 
 def send_over(x, flip):
@@ -760,12 +795,7 @@
     return lax.ppermute(x, "dp", [(0, 1), (1, 0)])
 
 
-def sum_start(x):
-    half = x.shape[0] // 2
-    dp = lax.axis_index("dp")
-    mine = lax.dynamic_slice_in_dim(x, dp * half, half, 0)
-    other = lax.dynamic_slice_in_dim(x, (1 - dp) * half, half, 0)
-    chip = (mine.astype(F32) + swap_cores(other).astype(F32)).astype(BF16)
+def sum_start(chip):
     sent = [chip]
     for flip in (1, 2, 3):
         sent.append(send_over(chip, flip))
@@ -777,12 +807,6 @@
     other = swap_cores(total)
     first = lax.axis_index("dp") == 0
     return jnp.concatenate([jnp.where(first, total, other), jnp.where(first, other, total)], axis=0)
-
-
-def dense_finish(grad_y, routed, shared, act, w_dense):
-    grad_mixed = (grad_y.astype(F32) + routed + shared).astype(BF16)
-    grad_act = (grad_mixed.astype(F32) + dot_nn(w_dense, grad_mixed)).astype(BF16)
-    return grad_act, dot_nt(act, grad_mixed).astype(BF16)
 
 
 def solution(mesh):
@@ -808,24 +832,22 @@
 
         x1 = act_in.T
         grad_y2 = grad_out.T
-        shared_w = [(ws_gate[layer], ws_up[layer], jnp.swapaxes(ws_down[layer], 0, 1)) for layer in range(layers)]
-        tok1, metas, u1 = first_exchange(x1, w_dense[0], meta)
+        shared_w = (ws_gate, ws_up, jnp.swapaxes(ws_down, 1, 2))
+        tok1, metas, u1 = first_exchange(x1, w_dense, meta)
         tok1, grad_y2 = lax.optimization_barrier((tok1, grad_y2))
         grads2 = [grad_y2, send_over(grad_y2, 1), send_over(grad_y2, 2), send_over(grad_y2, 3)]
         grads2 = grads2 + [swap_cores(x) for x in grads2]
-        meta1, meta2 = metas[:, : 2 * top], metas[:, 2 * top :]
-        part, rows1 = expert_forward(0, capacity, groups, base, tok1, meta1, w_gate, w_up, w_down_t)
-        tok2, x2, u2 = forward_exchange(part, u1, *shared_w[0], w_dense[1])
-        back2, *held = expert_backward(1, capacity, groups, base, tok2, False, grads2, meta2, w_gate, w_up, w_down_t, [])
-        grad1_all, recv2, grad_y1, shared1, early = backward_exchange(back2, held, grad_y2, x2, u2, u1, w_dense[1], shared_w[1], shared_w[0])
+        part, rows1 = expert_forward(0, capacity, groups, base, tok1, metas, w_gate, w_up, w_down_t)
+        tok2, x2, u2 = forward_exchange(part, u1, *shared_w, w_dense)
+        back2, *held = expert_backward(1, capacity, groups, base, tok2, False, grads2, metas, w_gate, w_up, w_down_t, [])
+        grad1_all, recv2, grad_y1, shared1, early = backward_exchange(back2, held, grad_y2, x2, u2, u1, w_dense, *shared_w)
         ff = ws_gate.shape[2]
         width = w_dense.shape[1]
         early = sum_start(early)
         grad1_all, early[0] = lax.optimization_barrier((grad1_all, early[0]))
-        back1, *held = expert_backward(0, capacity, groups, base, rows1, True, [grad1_all], meta1, w_gate, w_up, w_down_t, [recv2] + held)
-        routed1, recv1 = last_exchange(back1, held)
-        grad_x, g_w_dense1 = dense_finish(grad_y1, routed1, shared1, x1, w_dense[0])
-        late = sum_start(g_w_dense1)
+        back1, *held = expert_backward(0, capacity, groups, base, rows1, True, [grad1_all], metas, w_gate, w_up, w_down_t, [recv2] + held)
+        grad_x, recv1, late = last_exchange(back1, held, grad_y1, shared1, x1, w_dense)
+        late = sum_start(late)
         g_gate, g_up, g_down = place(0, groups, base, recv1, held)
         g_gate, late = lax.optimization_barrier((g_gate, late))
         g_down = jnp.swapaxes(g_down, 2, 3)

time: 479 us -> 473 us (0.987)
  local copies, waits for them, and re-layouts: 8.7 us -> 1.69 us
  Pallas kernels: 423 us -> 430 us
  transfers between devices with their start and end apart: 17 -> 15, of which waited for: 5 -> 3; matrix products, arithmetic and copies ran while one was open for 2% -> 0% of each run, Pallas kernels for 35% -> 36%
where the time goes in v2:
time: 473 us; the launch traced here: 472 us
  Pallas kernels  430 us (91%)
  waiting for transfers between devices  20.1 us (4%)
  starting transfers between devices  11 us (2%)
  other arithmetic  8.32 us (2%)
    pallas_call x4, Pallas kernels, comm_call(): pl.pallas_call(kernel, out_shape=out_shape, in_specs=in_specs, out_specs=...  210 us
    pallas_call x2, Pallas kernels, expert_backward(): pl.pallas_call(functools.partial(bwd_kernel, layer, capacity, groups, len...  130 us
    pallas_call x1, Pallas kernels, expert_forward(): pl.pallas_call(functools.partial(fwd_kernel, layer, capacity, groups), ou...  77 us
    ppermute x9, waiting for transfers between devices, send_over(): return lax.ppermute(x, 'ep', [(i, i ^ flip) for i in range(4)])  18.9 us
    pallas_call x1, Pallas kernels, place(): pl.pallas_call(place_kernel, out_shape=(shape, shape, shape), grid_spec=p...  13.3 us
    ppermute x9, starting transfers between devices, send_over(): return lax.ppermute(x, 'ep', [(i, i ^ flip) for i in range(4)])  9.8 us
  transfers between devices with their start and end apart: 15, of which 3 were waited for; matrix products, arithmetic and copies ran while one was open for 0% of the time, Pallas kernels for 36%

profile of v2, /device:TPU:0, one launch (start us, length us, event | category | flops | bytes accessed | tf_op | source)
XLA Modules:
  0.0 472.1 jit_solution(12778824903064190101)
XLA Ops:
  0.6 0.8 convert_bitcast_fusion
  1.4 1.4 pad_maximum_fusion.4
  2.9 37.0 %shard_map.170 = (bf16[8,448,768]{2,1,0:T(8,128)(2,1)}, f32[8,32,768]{2,1,0:T(8,128)}, bf16[448,768]{1,0:T(8,128)(2,1)}) custom-call(bf16[448,768]{1,0:T(8,128)(2,1)} %bitcast.42, bf16[2,448,448]{2,1,0:T(8,128)(2,1)} %w_dense_ref.7, f32[32,768]{1,0:T(8,128)} %bitcast.46), custom_call_target="tpu_custom_call" | custom-call | flops 20000000000 | bytes 20000000 | tf_op jit(solution)/shard_map/pallas_call | solution.py:650
  39.9 0.1 collective-permute-start.3
  40.0 1.5 collective-permute-start.2
  41.5 1.0 collective-permute-start.1
  42.5 1.1 collective-permute-start
  43.5 0.6 pad_add_fusion.base_ref
  44.1 77.0 %shard_map.171 = (f32[8,448,768]{2,1,0:T(8,128)}, bf16[6,8,256,480]{3,2,1,0:T(8,128)(2,1)}) custom-call(s32[3]{0:T(128)} %pad_add_fusion.base_ref, f32[8,32,768]{2,1,0:T(8,128)} %get-tuple-element.44.meta_ref, bf16[2,96,448,128]{3,2,1,0:T(8,128)(2,1)} %w1_ref.5, bf16[2,96,448,128]{3,2,1,0:T(8,128)(2,1)} %w3_ref.5, bf16[2,96,448,128]{3,2,1,0:T(8,128)(2,1)} %bitcast.32, ...), custom_call_target="tpu_custom_call" | custom-call | flops 20000000000 | bytes 20000000 | tf_op jit(solution)/shard_map/pallas_call | solution.py:364
  121.1 0.0 collective-permute-done.2.refs_4_
  121.1 0.0 collective-permute-start.6
  121.1 0.0 collective-permute-done.1.refs_3_
  121.1 0.5 collective-permute-start.5
  121.6 0.0 collective-permute-done.refs_2_
  121.6 0.0 collective-permute-start.4
  121.7 80.1 %shard_map.172 = (bf16[8,448,768]{2,1,0:T(8,128)(2,1)}, bf16[448,768]{1,0:T(8,128)(2,1)}, bf16[448,768]{1,0:T(8,128)(2,1)}) custom-call(f32[8,448,768]{2,1,0:T(8,128)} %get-tuple-element.48.part_ref, bf16[448,768]{1,0:T(8,128)(2,1)} %get-tuple-element.49.u1_ref, bf16[2,448,128]{2,1,0:T(8,128)(2,1)} %ws_gate_ref.3, bf16[2,448,128]{2,1,0:T(8,128)(2,1)} %ws_up_ref.3, ...), custom_call_target="tpu_custom_call" | custom-call | flops 20000000000 | bytes 20000000 | tf_op jit(solution)/shard_map/pallas_call | solution.py:650
  201.8 0.0 collective-permute-done.3.refs_5_
  201.8 0.0 copy-start.2
  201.8 0.0 collective-permute-done.6.refs_8_
  201.8 0.0 collective-permute-done.5.refs_7_
  201.8 0.8 copy-done.2
  202.6 68.0 %shard_map.173 = (bf16[8,448,768]{2,1,0:T(8,128)(2,1)}, bf16[2,96,448,128]{3,2,1,0:T(8,128)(2,1)}, bf16[2,96,448,128]{3,2,1,0:T(8,128)(2,1)}, bf16[2,96,448,128]{3,2,1,0:T(8,128)(2,1)}) custom-call(s32[3]{0:T(128)} %pad_add_fusion.base_ref, f32[8,32,768]{2,1,0:T(8,128)} %get-tuple-element.44.meta_ref, bf16[2,96,448,128]{3,2,1,0:T(8,128)(2,1)} %w1_ref.5, ...), custom_call_target="tpu_custom_call" | custom-call | flops 20000000000 | bytes 20000000 | tf_op jit(solution)/shard_map/pallas_call | solution.py:401
  270.6 58.5 %shard_map.174 = (bf16[8,448,768]{2,1,0:T(8,128)(2,1)}, bf16[3,48,448,128]{3,2,1,0:T(8,128)(2,1)}, bf16[448,768]{1,0:T(8,128)(2,1)}, f32[448,768]{1,0:T(8,128)}, bf16[224,1280]{1,0:T(8,128)(2,1)}) custom-call(bf16[8,448,768]{2,1,0:T(8,128)(2,1)} %get-tuple-element.52.part_ref, bf16[2,96,448,128]{3,2,1,0:T(8,128)(2,1)} %get-tuple-element.53.d1_ref.refs_3_, ...), custom_call_target="tpu_custom_call" | custom-call | flops 20000000000 | bytes 20000000 | tf_op jit(solution)/shard_map/pallas_call | solution.py:650
  329.1 61.8 %shard_map.175 = (bf16[8,448,768]{2,1,0:T(8,128)(2,1)}, bf16[2,96,448,128]{3,2,1,0:T(8,128)(2,1)}, bf16[2,96,448,128]{3,2,1,0:T(8,128)(2,1)}, bf16[2,96,448,128]{3,2,1,0:T(8,128)(2,1)}) custom-call(s32[3]{0:T(128)} %pad_add_fusion.base_ref, f32[8,32,768]{2,1,0:T(8,128)} %get-tuple-element.44.meta_ref, ...), custom_call_target="tpu_custom_call", output_to_operand_aliasing={{1}: (8, {}), {2}: (9, {}), {3}: (10, {})} | custom-call | flops 20000000000 | bytes 20000000 | tf_op jit(solution)/shard_map/pallas_call | solution.py:401
  390.9 34.5 %shard_map.176 = (bf16[448,768]{1,0:T(8,128)(2,1)}, bf16[3,48,448,128]{3,2,1,0:T(8,128)(2,1)}, bf16[224,448]{1,0:T(8,128)(2,1)}) custom-call(bf16[8,448,768]{2,1,0:T(8,128)(2,1)} %get-tuple-element.62.part_ref, bf16[2,96,448,128]{3,2,1,0:T(8,128)(2,1)} %get-tuple-element.63.d1_ref.refs_0_, bf16[2,96,448,128]{3,2,1,0:T(8,128)(2,1)} %get-tuple-element.64.d3_ref.refs_1_, ...), custom_call_target="tpu_custom_call" | custom-call | flops 20000000000 | bytes 20000000 | tf_op jit(solution)/shard_map/pallas_call | solution.py:650
  425.4 1.5 collective-permute-start.9
  426.9 1.5 collective-permute-start.13
  428.4 0.7 collective-permute-start.12
  429.1 1.4 collective-permute-start.11
  430.4 0.7 collective-permute-start.8
  431.1 4.1 collective-permute-done.9
  435.1 0.7 collective-permute-start.7
  435.8 0.0 copy-done.5
  435.8 13.3 %shard_map.177 = (bf16[2,96,448,128]{3,2,1,0:T(8,128)(2,1)}, bf16[2,96,448,128]{3,2,1,0:T(8,128)(2,1)}, bf16[2,96,448,128]{3,2,1,0:T(8,128)(2,1)}) custom-call(s32[3]{0:T(128)} %pad_add_fusion.base_ref, bf16[3,48,448,128]{3,2,1,0:T(8,128)(2,1)} %get-tuple-element.69.recv_ref, ...), custom_call_target="tpu_custom_call", output_to_operand_aliasing={{0}: (2, {}), {1}: (3, {}), {2}: (4, {})} | custom-call | flops 20000000000 | bytes 20000000 | tf_op jit(solution)/shard_map/pallas_call | solution.py:441
  449.2 14.9 %collective-permute-done.8 = bf16[224,448]{1,0:T(8,128)(2,1)} collective-permute-done((bf16[224,448]{1,0:T(8,128)(2,1)}, bf16[224,448]{1,0:T(8,128)(2,1)}, u32[]{:S(2)}, u32[]{:S(2)}) %collective-permute-start.8) | collective-permute-done | bytes 200736 | tf_op jit(solution)/shard_map/ppermute | solution.py:791
  464.0 0.0 collective-permute-done.7
  464.0 0.0 collective-permute-done.13
  464.1 1.3 add_convert_fusion
  465.4 0.0 collective-permute-start.14
  465.5 1.3 add_convert_fusion.1
  466.7 0.5 collective-permute-start.10
  467.3 1.1 collective-permute-done.10
  468.5 0.1 broadcast_select_fusion
  468.6 0.1 fusion.12
  468.7 0.7 maximum_bitcast_fusion.1
  469.4 1.0 pad_maximum_fusion
  470.5 0.8 pad_maximum_fusion.1
  471.3 0.8 copy.32
  (16 shorter events, 0.1 us)
Async XLA Ops:
  2.9 37.0 %copy-start = (bf16[768,448]{0,1:T(8,128)(2,1)S(1)}, bf16[768,448]{0,1:T(8,128)(2,1)}, u32[]{:S(2)}) copy-start(bf16[768,448]{0,1:T(8,128)(2,1)} %param.12) | copy-start | bytes 2064388
  39.9 161.9 %collective-permute-start.3 = (bf16[448,768]{1,0:T(8,128)(2,1)S(1)}, bf16[448,768]{1,0:T(8,128)(2,1)S(1)}, u32[]{:S(2)}, u32[]{:S(2)}) collective-permute-start(bf16[448,768]{1,0:T(8,128)(2,1)S(1)} %bitcast.37), channel_id=1, source_target_pairs={{0,1},{1,0},{2,3},{3,2},{4,5},{5,4},{6,7},{7,6}} | collective-permute-start | bytes 2064392 | tf_op jit(solution)/shard_map/ppermute | solution.py:795
  40.0 81.0 %collective-permute-start.2 = (bf16[448,768]{1,0:T(8,128)(2,1)S(1)}, bf16[448,768]{1,0:T(8,128)(2,1)}, u32[]{:S(2)}, u32[]{:S(2)}) collective-permute-start(bf16[448,768]{1,0:T(8,128)(2,1)S(1)} %bitcast.38), channel_id=1, source_target_pairs={{0,6},{2,4},{4,2},{6,0},{1,7},{3,5},{5,3},{7,1}} | collective-permute-start | bytes 2064392 | tf_op jit(solution)/shard_map/ppermute | solution.py:791
  41.5 79.6 %collective-permute-start.1 = (bf16[448,768]{1,0:T(8,128)(2,1)S(1)}, bf16[448,768]{1,0:T(8,128)(2,1)}, u32[]{:S(2)}, u32[]{:S(2)}) collective-permute-start(bf16[448,768]{1,0:T(8,128)(2,1)S(1)} %bitcast.39), channel_id=1, source_target_pairs={{0,4},{2,6},{4,0},{6,2},{1,5},{3,7},{5,1},{7,3}} | collective-permute-start | bytes 2064392 | tf_op jit(solution)/shard_map/ppermute | solution.py:791
  42.5 79.2 %collective-permute-start = (bf16[448,768]{1,0:T(8,128)(2,1)S(1)}, bf16[448,768]{1,0:T(8,128)(2,1)}, u32[]{:S(2)}, u32[]{:S(2)}) collective-permute-start(bf16[448,768]{1,0:T(8,128)(2,1)S(1)} %bitcast.40), channel_id=1, source_target_pairs={{0,2},{2,0},{4,6},{6,4},{1,3},{3,1},{5,7},{7,5}} | collective-permute-start | bytes 2064392 | tf_op jit(solution)/shard_map/ppermute | solution.py:791
  121.1 80.7 %collective-permute-start.6 = (bf16[448,768]{1,0:T(8,128)(2,1)}, bf16[448,768]{1,0:T(8,128)(2,1)}, u32[]{:S(2)}, u32[]{:S(2)}) collective-permute-start(bf16[448,768]{1,0:T(8,128)(2,1)} %collective-permute-done.2.refs_4_), channel_id=1, source_target_pairs={{0,1},{1,0},{2,3},{3,2},{4,5},{5,4},{6,7},{7,6}} | collective-permute-start | bytes 2064392 | tf_op jit(solution)/shard_map/ppermute | solution.py:795
  121.1 80.7 %collective-permute-start.5 = (bf16[448,768]{1,0:T(8,128)(2,1)}, bf16[448,768]{1,0:T(8,128)(2,1)}, u32[]{:S(2)}, u32[]{:S(2)}) collective-permute-start(bf16[448,768]{1,0:T(8,128)(2,1)} %collective-permute-done.1.refs_3_), channel_id=1, source_target_pairs={{0,1},{1,0},{2,3},{3,2},{4,5},{5,4},{6,7},{7,6}} | collective-permute-start | bytes 2064392 | tf_op jit(solution)/shard_map/ppermute | solution.py:795
  121.6 80.2 %collective-permute-start.4 = (bf16[448,768]{1,0:T(8,128)(2,1)}, bf16[448,768]{1,0:T(8,128)(2,1)}, u32[]{:S(2)}, u32[]{:S(2)}) collective-permute-start(bf16[448,768]{1,0:T(8,128)(2,1)} %collective-permute-done.refs_2_), channel_id=1, source_target_pairs={{0,1},{1,0},{2,3},{3,2},{4,5},{5,4},{6,7},{7,6}} | collective-permute-start | bytes 2064392 | tf_op jit(solution)/shard_map/ppermute | solution.py:795
  201.8 0.8 copy-start.2
  390.9 36.0 %copy-start.3 = (bf16[224,1280]{1,0:T(8,128)(2,1)S(1)}, bf16[224,1280]{1,0:T(8,128)(2,1)}, u32[]{:S(2)}) copy-start(bf16[224,1280]{1,0:T(8,128)(2,1)} %get-tuple-element.76) | copy-start | bytes 1720324
  425.4 9.7 %collective-permute-start.9 = (bf16[224,448]{1,0:T(8,128)(2,1)}, bf16[224,448]{1,0:T(8,128)(2,1)S(1)}, u32[]{:S(2)}, u32[]{:S(2)}) collective-permute-start(bf16[224,448]{1,0:T(8,128)(2,1)} %get-tuple-element.72), channel_id=1, source_target_pairs={{0,6},{2,4},{4,2},{6,0},{1,7},{3,5},{5,3},{7,1}} | collective-permute-start | bytes 602120 | tf_op jit(solution)/shard_map/ppermute | solution.py:791
  426.9 37.1 %collective-permute-start.13 = (bf16[224,1280]{1,0:T(8,128)(2,1)S(1)}, bf16[224,1280]{1,0:T(8,128)(2,1)S(1)}, u32[]{:S(2)}, u32[]{:S(2)}) collective-permute-start(bf16[224,1280]{1,0:T(8,128)(2,1)S(1)} %copy-done.3), channel_id=1, source_target_pairs={{0,6},{2,4},{4,2},{6,0},{1,7},{3,5},{5,3},{7,1}} | collective-permute-start | bytes 1720328 | tf_op jit(solution)/shard_map/ppermute | solution.py:791
  428.4 35.7 %collective-permute-start.12 = (bf16[224,1280]{1,0:T(8,128)(2,1)S(1)}, bf16[224,1280]{1,0:T(8,128)(2,1)S(1)}, u32[]{:S(2)}, u32[]{:S(2)}) collective-permute-start(bf16[224,1280]{1,0:T(8,128)(2,1)S(1)} %copy-done.3), channel_id=1, source_target_pairs={{0,4},{2,6},{4,0},{6,2},{1,5},{3,7},{5,1},{7,3}} | collective-permute-start | bytes 1720328 | tf_op jit(solution)/shard_map/ppermute | solution.py:791
  429.1 35.0 %collective-permute-start.11 = (bf16[224,1280]{1,0:T(8,128)(2,1)S(1)}, bf16[224,1280]{1,0:T(8,128)(2,1)}, u32[]{:S(2)}, u32[]{:S(2)}) collective-permute-start(bf16[224,1280]{1,0:T(8,128)(2,1)S(1)} %copy-done.3), channel_id=1, source_target_pairs={{0,2},{2,0},{4,6},{6,4},{1,3},{3,1},{5,7},{7,5}} | collective-permute-start | bytes 1720328 | tf_op jit(solution)/shard_map/ppermute | solution.py:791
  430.4 33.6 %collective-permute-start.8 = (bf16[224,448]{1,0:T(8,128)(2,1)}, bf16[224,448]{1,0:T(8,128)(2,1)}, u32[]{:S(2)}, u32[]{:S(2)}) collective-permute-start(bf16[224,448]{1,0:T(8,128)(2,1)} %get-tuple-element.72), channel_id=1, source_target_pairs={{0,4},{2,6},{4,0},{6,2},{1,5},{3,7},{5,1},{7,3}} | collective-permute-start | bytes 602120 | tf_op jit(solution)/shard_map/ppermute | solution.py:791
  435.1 0.7 copy-start.5
  435.1 28.9 %collective-permute-start.7 = (bf16[224,448]{1,0:T(8,128)(2,1)}, bf16[224,448]{1,0:T(8,128)(2,1)}, u32[]{:S(2)}, u32[]{:S(2)}) collective-permute-start(bf16[224,448]{1,0:T(8,128)(2,1)} %get-tuple-element.72), channel_id=1, source_target_pairs={{0,2},{2,0},{4,6},{6,4},{1,3},{3,1},{5,7},{7,5}} | collective-permute-start | bytes 602120 | tf_op jit(solution)/shard_map/ppermute | solution.py:791
  435.8 29.6 %copy-start.4 = (bf16[224,448]{1,0:T(8,128)(2,1)S(1)}, bf16[224,448]{1,0:T(8,128)(2,1)}, u32[]{:S(2)}) copy-start(bf16[224,448]{1,0:T(8,128)(2,1)} %get-tuple-element.72) | copy-start | bytes 602116
  465.4 3.1 collective-permute-start.14
  466.7 4.5 copy-start.1
  466.7 1.6 collective-permute-start.10

commit v3 on v2

--- a/solution.py
+++ b/solution.py
@@ -38,7 +38,7 @@
     return pre_act * sigma, sigma * (1.0 + pre_act * (1.0 - sigma))
 
 
-def route(meta_ref, layer, src, first_expert, capacity, pick_ref, slot, tok_ref=None):
+def route(meta_ref, layer, src, first_expert, capacity, pick_ref, slot, tok_ref=None, weigh_ref=None):
     top = meta_ref.shape[1] // 4
     tokens = meta_ref.shape[2]
     start = 2 * layer * top
@@ -64,10 +64,15 @@
     rows = lax.broadcasted_iota(jnp.int32, (step, tokens), 0).astype(F32).astype(BF16)
     for k in range(GROUP):
         wanted = jnp.broadcast_to(row_of[k : k + 1, :], (step, tokens)).astype(BF16)
+        if weigh_ref is not None:
+            parts = [jnp.broadcast_to(part[k : k + 1, :].astype(F32), (step, tokens)).astype(BF16) for part in (high, middle, low)]
         for h in range(capacity // step):
             hit = wanted == rows + jnp.asarray(h * step, BF16)
             start = k * capacity + h * step
             pick_ref[slot, src, start : start + step, :] = jnp.where(hit, jnp.asarray(1, BF16), jnp.asarray(0, BF16))
+            if weigh_ref is not None:
+                for i, part in enumerate(parts):
+                    weigh_ref[slot, i, src, start : start + step, :] = jnp.where(hit, part, jnp.asarray(0, BF16))
 
 
 def gate_column(found, capacity):
@@ -129,7 +134,7 @@
         copy.wait()
 
 
-def fwd_kernel(layer, capacity, groups, base_ref, meta_ref, w1_ref, w3_ref, w2_ref, tokens_ref, out_ref, xs_ref, sum_ref, tok_ref, pick_ref, gate_ref, x_ref, o_ref, sem, out_sem, save_sem):
+def fwd_kernel(layer, capacity, groups, base_ref, meta_ref, w1_ref, w3_ref, w2_ref, tokens_ref, out_ref, xs_ref, sum_ref, tok_ref, pick_ref, weigh_ref, x_ref, o_ref, sem, out_sem, save_sem):
     group = pl.program_id(0)
     sources = tok_ref.shape[0]
     width = w1_ref.shape[1]
@@ -144,10 +149,9 @@
             load(src).start()
 
     def dispatch(src):
-        route(meta_ref, layer, src, base_ref[0] + group * GROUP, capacity, pick_ref, now, tok_ref)
+        route(meta_ref, layer, src, base_ref[0] + group * GROUP, capacity, pick_ref, now, tok_ref, weigh_ref)
         found = dot_nt(pick_ref[now, src], tok_ref[src])
         x_ref[now, src] = found.astype(BF16)
-        gate_ref[src] = gate_column(found, capacity)
 
     def expert(k):
         here = pl.ds(pl.multiple_of(k * capacity, capacity), capacity)
@@ -155,18 +159,11 @@
         ff = w1_ref.shape[2]
         a = dot_nn(x, jnp.concatenate([w1_ref[k], w3_ref[k]], axis=1))
         hidden = (jax.nn.silu(a[:, :ff]) * a[:, ff:]).astype(BF16)
-        out = dot_nt(hidden, w2_ref[k]).astype(BF16).astype(F32)
-        gate = gate_ref[:, here, :].reshape(sources * capacity, 1)
-        o_ref[:, here, :] = (gate * out).reshape(sources, capacity, width)
+        o_ref[:, here, :] = dot_nt(hidden, w2_ref[k]).astype(BF16).reshape(sources, capacity, width)
 
     def added(src):
-        rest = o_ref[src].T
-        pick = pick_ref[before, src]
-        parts = []
-        for _ in range(3):
-            parts.append(rest.astype(BF16))
-            rest = rest - parts[-1].astype(F32)
-        return dot_nn(parts[0], pick) + dot_nn(parts[1], pick) + dot_nn(parts[2], pick)
+        rows = o_ref[src]
+        return dot_tn(rows, weigh_ref[before, 0, src]) + dot_tn(rows, weigh_ref[before, 1, src]) + dot_tn(rows, weigh_ref[before, 2, src])
 
     def combine(src):
         @pl.when(group == 1)
@@ -376,9 +373,9 @@
                 pltpu.VMEM((sources, width, tokens), F32),
                 pltpu.VMEM((sources, width + 4 * GROUP, tokens), BF16),
                 pltpu.VMEM((2, sources, rows, tokens), BF16),
-                pltpu.VMEM((sources, rows, 1), F32),
+                pltpu.VMEM((2, 3, sources, rows, tokens), BF16),
                 pltpu.VMEM((2, sources, rows, width + 4 * GROUP), BF16),
-                pltpu.VMEM((sources, rows, width), F32),
+                pltpu.VMEM((sources, rows, width), BF16),
                 pltpu.SemaphoreType.DMA((sources,)),
                 pltpu.SemaphoreType.DMA((sources,)),
                 pltpu.SemaphoreType.DMA((2, 1)),

time: 473 us -> 459 us (0.970)
  Pallas kernels: 430 us -> 417 us
    pallas_call x1, Pallas kernels: 77 us -> 63.3 us  [expert_forward(): pl.pallas_call(functools.partial(fwd_kernel, layer, capacity, groups), ou...]
  transfers between devices with their start and end apart: 15 -> 15, of which waited for: 3 -> 3; matrix products, arithmetic and copies ran while one was open for 0% -> 0% of each run, Pallas kernels for 36% -> 34%
where the time goes in v3:
time: 459 us
  Pallas kernels  417 us (91%)
  waiting for transfers between devices  20.1 us (4%)
  starting transfers between devices  11 us (2%)
  other arithmetic  8.32 us (2%)
    pallas_call x4, Pallas kernels, comm_call(): pl.pallas_call(kernel, out_shape=out_shape, in_specs=in_specs, out_specs=...  210 us
    pallas_call x2, Pallas kernels, expert_backward(): pl.pallas_call(functools.partial(bwd_kernel, layer, capacity, groups, len...  130 us
    pallas_call x1, Pallas kernels, expert_forward(): pl.pallas_call(functools.partial(fwd_kernel, layer, capacity, groups), ou...  63.3 us
    ppermute x9, waiting for transfers between devices, send_over(): return lax.ppermute(x, 'ep', [(i, i ^ flip) for i in range(4)])  19 us
    pallas_call x1, Pallas kernels, place(): pl.pallas_call(place_kernel, out_shape=(shape, shape, shape), grid_spec=p...  13.3 us
    ppermute x9, starting transfers between devices, send_over(): return lax.ppermute(x, 'ep', [(i, i ^ flip) for i in range(4)])  9.76 us
  transfers between devices with their start and end apart: 15, of which 3 were waited for; matrix products, arithmetic and copies ran while one was open for 0% of the time, Pallas kernels for 34%

profile of v3, /device:TPU:0, one launch (start us, length us, event | category | flops | bytes accessed | tf_op | source)
XLA Modules:
  0.0 458.5 jit_solution(1369744312971441265)
XLA Ops:
  0.6 0.8 convert_bitcast_fusion
  1.4 1.4 pad_maximum_fusion.4
  2.9 37.0 %shard_map.170 = (bf16[8,448,768]{2,1,0:T(8,128)(2,1)}, f32[8,32,768]{2,1,0:T(8,128)}, bf16[448,768]{1,0:T(8,128)(2,1)}) custom-call(bf16[448,768]{1,0:T(8,128)(2,1)} %bitcast.42, bf16[2,448,448]{2,1,0:T(8,128)(2,1)} %w_dense_ref.7, f32[32,768]{1,0:T(8,128)} %bitcast.46), custom_call_target="tpu_custom_call" | custom-call | flops 20000000000 | bytes 20000000 | tf_op jit(solution)/shard_map/pallas_call | solution.py:647
  39.9 0.1 collective-permute-start.3
  40.0 1.5 collective-permute-start.2
  41.5 1.0 collective-permute-start.1
  42.5 1.1 collective-permute-start
  43.5 0.6 pad_add_fusion.base_ref
  44.1 63.3 %shard_map.171 = (f32[8,448,768]{2,1,0:T(8,128)}, bf16[6,8,256,480]{3,2,1,0:T(8,128)(2,1)}) custom-call(s32[3]{0:T(128)} %pad_add_fusion.base_ref, f32[8,32,768]{2,1,0:T(8,128)} %get-tuple-element.44.meta_ref, bf16[2,96,448,128]{3,2,1,0:T(8,128)(2,1)} %w1_ref.5, bf16[2,96,448,128]{3,2,1,0:T(8,128)(2,1)} %w3_ref.5, bf16[2,96,448,128]{3,2,1,0:T(8,128)(2,1)} %bitcast.32, ...), custom_call_target="tpu_custom_call" | custom-call | flops 20000000000 | bytes 20000000 | tf_op jit(solution)/shard_map/pallas_call | solution.py:361
  107.5 0.0 collective-permute-done.2.refs_4_
  107.5 0.0 collective-permute-start.6
  107.5 0.0 collective-permute-done.1.refs_3_
  107.5 0.5 collective-permute-start.5
  108.0 0.0 collective-permute-done.refs_2_
  108.0 0.0 collective-permute-start.4
  108.1 80.1 %shard_map.172 = (bf16[8,448,768]{2,1,0:T(8,128)(2,1)}, bf16[448,768]{1,0:T(8,128)(2,1)}, bf16[448,768]{1,0:T(8,128)(2,1)}) custom-call(f32[8,448,768]{2,1,0:T(8,128)} %get-tuple-element.48.part_ref, bf16[448,768]{1,0:T(8,128)(2,1)} %get-tuple-element.49.u1_ref, bf16[2,448,128]{2,1,0:T(8,128)(2,1)} %ws_gate_ref.3, bf16[2,448,128]{2,1,0:T(8,128)(2,1)} %ws_up_ref.3, ...), custom_call_target="tpu_custom_call" | custom-call | flops 20000000000 | bytes 20000000 | tf_op jit(solution)/shard_map/pallas_call | solution.py:647
  188.1 0.0 copy-start.2
  188.2 0.0 collective-permute-done.6.refs_8_
  188.2 0.0 collective-permute-done.4.refs_6_
  188.2 0.8 copy-done.2
  189.0 68.0 %shard_map.173 = (bf16[8,448,768]{2,1,0:T(8,128)(2,1)}, bf16[2,96,448,128]{3,2,1,0:T(8,128)(2,1)}, bf16[2,96,448,128]{3,2,1,0:T(8,128)(2,1)}, bf16[2,96,448,128]{3,2,1,0:T(8,128)(2,1)}) custom-call(s32[3]{0:T(128)} %pad_add_fusion.base_ref, f32[8,32,768]{2,1,0:T(8,128)} %get-tuple-element.44.meta_ref, bf16[2,96,448,128]{3,2,1,0:T(8,128)(2,1)} %w1_ref.5, ...), custom_call_target="tpu_custom_call" | custom-call | flops 20000000000 | bytes 20000000 | tf_op jit(solution)/shard_map/pallas_call | solution.py:398
  257.0 58.5 %shard_map.174 = (bf16[8,448,768]{2,1,0:T(8,128)(2,1)}, bf16[3,48,448,128]{3,2,1,0:T(8,128)(2,1)}, bf16[448,768]{1,0:T(8,128)(2,1)}, f32[448,768]{1,0:T(8,128)}, bf16[224,1280]{1,0:T(8,128)(2,1)}) custom-call(bf16[8,448,768]{2,1,0:T(8,128)(2,1)} %get-tuple-element.52.part_ref, bf16[2,96,448,128]{3,2,1,0:T(8,128)(2,1)} %get-tuple-element.53.d1_ref.refs_3_, ...), custom_call_target="tpu_custom_call" | custom-call | flops 20000000000 | bytes 20000000 | tf_op jit(solution)/shard_map/pallas_call | solution.py:647
  315.5 61.8 %shard_map.175 = (bf16[8,448,768]{2,1,0:T(8,128)(2,1)}, bf16[2,96,448,128]{3,2,1,0:T(8,128)(2,1)}, bf16[2,96,448,128]{3,2,1,0:T(8,128)(2,1)}, bf16[2,96,448,128]{3,2,1,0:T(8,128)(2,1)}) custom-call(s32[3]{0:T(128)} %pad_add_fusion.base_ref, f32[8,32,768]{2,1,0:T(8,128)} %get-tuple-element.44.meta_ref, ...), custom_call_target="tpu_custom_call", output_to_operand_aliasing={{1}: (8, {}), {2}: (9, {}), {3}: (10, {})} | custom-call | flops 20000000000 | bytes 20000000 | tf_op jit(solution)/shard_map/pallas_call | solution.py:398
  377.3 34.5 %shard_map.176 = (bf16[448,768]{1,0:T(8,128)(2,1)}, bf16[3,48,448,128]{3,2,1,0:T(8,128)(2,1)}, bf16[224,448]{1,0:T(8,128)(2,1)}) custom-call(bf16[8,448,768]{2,1,0:T(8,128)(2,1)} %get-tuple-element.62.part_ref, bf16[2,96,448,128]{3,2,1,0:T(8,128)(2,1)} %get-tuple-element.63.d1_ref.refs_0_, bf16[2,96,448,128]{3,2,1,0:T(8,128)(2,1)} %get-tuple-element.64.d3_ref.refs_1_, ...), custom_call_target="tpu_custom_call" | custom-call | flops 20000000000 | bytes 20000000 | tf_op jit(solution)/shard_map/pallas_call | solution.py:647
  411.8 1.5 collective-permute-start.9
  413.3 1.5 collective-permute-start.13
  414.8 0.6 collective-permute-start.12
  415.4 1.4 collective-permute-start.11
  416.8 0.7 collective-permute-start.8
  417.5 4.1 collective-permute-done.9
  421.5 0.7 collective-permute-start.7
  422.2 0.0 copy-done.5
  422.2 13.3 %shard_map.177 = (bf16[2,96,448,128]{3,2,1,0:T(8,128)(2,1)}, bf16[2,96,448,128]{3,2,1,0:T(8,128)(2,1)}, bf16[2,96,448,128]{3,2,1,0:T(8,128)(2,1)}) custom-call(s32[3]{0:T(128)} %pad_add_fusion.base_ref, bf16[3,48,448,128]{3,2,1,0:T(8,128)(2,1)} %get-tuple-element.69.recv_ref, ...), custom_call_target="tpu_custom_call", output_to_operand_aliasing={{0}: (2, {}), {1}: (3, {}), {2}: (4, {})} | custom-call | flops 20000000000 | bytes 20000000 | tf_op jit(solution)/shard_map/pallas_call | solution.py:438
  435.6 14.9 %collective-permute-done.8 = bf16[224,448]{1,0:T(8,128)(2,1)} collective-permute-done((bf16[224,448]{1,0:T(8,128)(2,1)}, bf16[224,448]{1,0:T(8,128)(2,1)}, u32[]{:S(2)}, u32[]{:S(2)}) %collective-permute-start.8) | collective-permute-done | bytes 200736 | tf_op jit(solution)/shard_map/ppermute | solution.py:788
  450.4 0.0 collective-permute-done.13
  450.4 0.0 collective-permute-done.12
  450.5 0.0 collective-permute-done.11
  450.5 1.3 add_convert_fusion
  451.8 0.0 collective-permute-start.14
  451.9 1.3 add_convert_fusion.1
  453.1 0.5 collective-permute-start.10
  453.6 1.1 collective-permute-done.10
  454.9 0.1 broadcast_select_fusion
  455.0 0.1 fusion.12
  455.1 0.7 maximum_bitcast_fusion.1
  455.8 1.0 pad_maximum_fusion
  456.9 0.8 pad_maximum_fusion.1
  457.7 0.8 copy.32
  (16 shorter events, 0.1 us)
Async XLA Ops:
  2.9 37.0 %copy-start = (bf16[768,448]{0,1:T(8,128)(2,1)S(1)}, bf16[768,448]{0,1:T(8,128)(2,1)}, u32[]{:S(2)}) copy-start(bf16[768,448]{0,1:T(8,128)(2,1)} %param.12) | copy-start | bytes 2064388
  39.9 148.2 %collective-permute-start.3 = (bf16[448,768]{1,0:T(8,128)(2,1)S(1)}, bf16[448,768]{1,0:T(8,128)(2,1)S(1)}, u32[]{:S(2)}, u32[]{:S(2)}) collective-permute-start(bf16[448,768]{1,0:T(8,128)(2,1)S(1)} %bitcast.37), channel_id=1, source_target_pairs={{0,1},{1,0},{2,3},{3,2},{4,5},{5,4},{6,7},{7,6}} | collective-permute-start | bytes 2064392 | tf_op jit(solution)/shard_map/ppermute | solution.py:792
  40.0 67.4 %collective-permute-start.2 = (bf16[448,768]{1,0:T(8,128)(2,1)S(1)}, bf16[448,768]{1,0:T(8,128)(2,1)}, u32[]{:S(2)}, u32[]{:S(2)}) collective-permute-start(bf16[448,768]{1,0:T(8,128)(2,1)S(1)} %bitcast.38), channel_id=1, source_target_pairs={{0,6},{2,4},{4,2},{6,0},{1,7},{3,5},{5,3},{7,1}} | collective-permute-start | bytes 2064392 | tf_op jit(solution)/shard_map/ppermute | solution.py:788
  41.5 66.0 %collective-permute-start.1 = (bf16[448,768]{1,0:T(8,128)(2,1)S(1)}, bf16[448,768]{1,0:T(8,128)(2,1)}, u32[]{:S(2)}, u32[]{:S(2)}) collective-permute-start(bf16[448,768]{1,0:T(8,128)(2,1)S(1)} %bitcast.39), channel_id=1, source_target_pairs={{0,4},{2,6},{4,0},{6,2},{1,5},{3,7},{5,1},{7,3}} | collective-permute-start | bytes 2064392 | tf_op jit(solution)/shard_map/ppermute | solution.py:788
  42.5 65.5 %collective-permute-start = (bf16[448,768]{1,0:T(8,128)(2,1)S(1)}, bf16[448,768]{1,0:T(8,128)(2,1)}, u32[]{:S(2)}, u32[]{:S(2)}) collective-permute-start(bf16[448,768]{1,0:T(8,128)(2,1)S(1)} %bitcast.40), channel_id=1, source_target_pairs={{0,2},{2,0},{4,6},{6,4},{1,3},{3,1},{5,7},{7,5}} | collective-permute-start | bytes 2064392 | tf_op jit(solution)/shard_map/ppermute | solution.py:788
  107.5 80.7 %collective-permute-start.6 = (bf16[448,768]{1,0:T(8,128)(2,1)}, bf16[448,768]{1,0:T(8,128)(2,1)}, u32[]{:S(2)}, u32[]{:S(2)}) collective-permute-start(bf16[448,768]{1,0:T(8,128)(2,1)} %collective-permute-done.2.refs_4_), channel_id=1, source_target_pairs={{0,1},{1,0},{2,3},{3,2},{4,5},{5,4},{6,7},{7,6}} | collective-permute-start | bytes 2064392 | tf_op jit(solution)/shard_map/ppermute | solution.py:792
  107.5 80.7 %collective-permute-start.5 = (bf16[448,768]{1,0:T(8,128)(2,1)}, bf16[448,768]{1,0:T(8,128)(2,1)}, u32[]{:S(2)}, u32[]{:S(2)}) collective-permute-start(bf16[448,768]{1,0:T(8,128)(2,1)} %collective-permute-done.1.refs_3_), channel_id=1, source_target_pairs={{0,1},{1,0},{2,3},{3,2},{4,5},{5,4},{6,7},{7,6}} | collective-permute-start | bytes 2064392 | tf_op jit(solution)/shard_map/ppermute | solution.py:792
  108.0 80.2 %collective-permute-start.4 = (bf16[448,768]{1,0:T(8,128)(2,1)}, bf16[448,768]{1,0:T(8,128)(2,1)}, u32[]{:S(2)}, u32[]{:S(2)}) collective-permute-start(bf16[448,768]{1,0:T(8,128)(2,1)} %collective-permute-done.refs_2_), channel_id=1, source_target_pairs={{0,1},{1,0},{2,3},{3,2},{4,5},{5,4},{6,7},{7,6}} | collective-permute-start | bytes 2064392 | tf_op jit(solution)/shard_map/ppermute | solution.py:792
  188.1 0.8 copy-start.2
  377.3 36.0 %copy-start.3 = (bf16[224,1280]{1,0:T(8,128)(2,1)S(1)}, bf16[224,1280]{1,0:T(8,128)(2,1)}, u32[]{:S(2)}) copy-start(bf16[224,1280]{1,0:T(8,128)(2,1)} %get-tuple-element.76) | copy-start | bytes 1720324
  411.8 9.7 %collective-permute-start.9 = (bf16[224,448]{1,0:T(8,128)(2,1)}, bf16[224,448]{1,0:T(8,128)(2,1)S(1)}, u32[]{:S(2)}, u32[]{:S(2)}) collective-permute-start(bf16[224,448]{1,0:T(8,128)(2,1)} %get-tuple-element.72), channel_id=1, source_target_pairs={{0,6},{2,4},{4,2},{6,0},{1,7},{3,5},{5,3},{7,1}} | collective-permute-start | bytes 602120 | tf_op jit(solution)/shard_map/ppermute | solution.py:788
  413.3 37.1 %collective-permute-start.13 = (bf16[224,1280]{1,0:T(8,128)(2,1)S(1)}, bf16[224,1280]{1,0:T(8,128)(2,1)S(1)}, u32[]{:S(2)}, u32[]{:S(2)}) collective-permute-start(bf16[224,1280]{1,0:T(8,128)(2,1)S(1)} %copy-done.3), channel_id=1, source_target_pairs={{0,6},{2,4},{4,2},{6,0},{1,7},{3,5},{5,3},{7,1}} | collective-permute-start | bytes 1720328 | tf_op jit(solution)/shard_map/ppermute | solution.py:788
  414.8 35.7 %collective-permute-start.12 = (bf16[224,1280]{1,0:T(8,128)(2,1)S(1)}, bf16[224,1280]{1,0:T(8,128)(2,1)S(1)}, u32[]{:S(2)}, u32[]{:S(2)}) collective-permute-start(bf16[224,1280]{1,0:T(8,128)(2,1)S(1)} %copy-done.3), channel_id=1, source_target_pairs={{0,4},{2,6},{4,0},{6,2},{1,5},{3,7},{5,1},{7,3}} | collective-permute-start | bytes 1720328 | tf_op jit(solution)/shard_map/ppermute | solution.py:788
  415.4 35.0 %collective-permute-start.11 = (bf16[224,1280]{1,0:T(8,128)(2,1)S(1)}, bf16[224,1280]{1,0:T(8,128)(2,1)}, u32[]{:S(2)}, u32[]{:S(2)}) collective-permute-start(bf16[224,1280]{1,0:T(8,128)(2,1)S(1)} %copy-done.3), channel_id=1, source_target_pairs={{0,2},{2,0},{4,6},{6,4},{1,3},{3,1},{5,7},{7,5}} | collective-permute-start | bytes 1720328 | tf_op jit(solution)/shard_map/ppermute | solution.py:788
  416.8 33.6 %collective-permute-start.8 = (bf16[224,448]{1,0:T(8,128)(2,1)}, bf16[224,448]{1,0:T(8,128)(2,1)}, u32[]{:S(2)}, u32[]{:S(2)}) collective-permute-start(bf16[224,448]{1,0:T(8,128)(2,1)} %get-tuple-element.72), channel_id=1, source_target_pairs={{0,4},{2,6},{4,0},{6,2},{1,5},{3,7},{5,1},{7,3}} | collective-permute-start | bytes 602120 | tf_op jit(solution)/shard_map/ppermute | solution.py:788
  421.5 0.7 copy-start.5
  421.5 28.9 %collective-permute-start.7 = (bf16[224,448]{1,0:T(8,128)(2,1)}, bf16[224,448]{1,0:T(8,128)(2,1)}, u32[]{:S(2)}, u32[]{:S(2)}) collective-permute-start(bf16[224,448]{1,0:T(8,128)(2,1)} %get-tuple-element.72), channel_id=1, source_target_pairs={{0,2},{2,0},{4,6},{6,4},{1,3},{3,1},{5,7},{7,5}} | collective-permute-start | bytes 602120 | tf_op jit(solution)/shard_map/ppermute | solution.py:788
  422.2 29.6 %copy-start.4 = (bf16[224,448]{1,0:T(8,128)(2,1)S(1)}, bf16[224,448]{1,0:T(8,128)(2,1)}, u32[]{:S(2)}) copy-start(bf16[224,448]{1,0:T(8,128)(2,1)} %get-tuple-element.72) | copy-start | bytes 602116
  451.8 3.1 collective-permute-start.14
  453.1 4.5 copy-start.1
  453.1 1.6 collective-permute-start.10

commit v4 on v3

--- a/solution.py
+++ b/solution.py
@@ -148,6 +148,10 @@
         for src in range(sources):
             load(src).start()
 
+    def wait(src):
+        load(src).wait()
+        sum_ref[src] = jnp.zeros(sum_ref.shape[1:], F32)
+
     def dispatch(src):
         route(meta_ref, layer, src, base_ref[0] + group * GROUP, capacity, pick_ref, now, tok_ref, weigh_ref)
         found = dot_nt(pick_ref[now, src], tok_ref[src])
@@ -166,10 +170,6 @@
         return dot_tn(rows, weigh_ref[before, 0, src]) + dot_tn(rows, weigh_ref[before, 1, src]) + dot_tn(rows, weigh_ref[before, 2, src])
 
     def combine(src):
-        @pl.when(group == 1)
-        def _():
-            sum_ref[src] = jnp.zeros(sum_ref.shape[1:], F32)
-
         sum_ref[src] += added(src)
 
     def store(src):
@@ -187,7 +187,7 @@
     def _():
         wait_all(saves(group - 2))
 
-    schedule(groups, sources, begin, lambda src: load(src).wait(), dispatch, expert, combine, finish)
+    schedule(groups, sources, begin, wait, dispatch, expert, combine, finish)
 
     @pl.when(group < groups)
     def _():
@@ -235,6 +235,7 @@
         if not keeps:
             load(src).wait()
         pltpu.make_async_copy(grad_ref.at[src], grad_ref.at[src], grad_sem.at[src]).wait()
+        sum_ref[src] = jnp.zeros(sum_ref.shape[1:], F32)
 
     def dispatch(src):
         if keeps:
@@ -280,10 +281,6 @@
         return dot_tn(r_ref[src], pick_ref[before, src])
 
     def combine(src):
-        @pl.when(group == 1)
-        def _():
-            sum_ref[src] = jnp.zeros(sum_ref.shape[1:], F32)
-
         sum_ref[src] += added(src)
 
     def store(src):

time: 459 us -> 459 us (level)
  no operation moved by 1% of the time
where the time goes in v4:
time: 459 us
  Pallas kernels  417 us (91%)
  waiting for transfers between devices  20.1 us (4%)
  starting transfers between devices  11 us (2%)
  other arithmetic  8.32 us (2%)
    pallas_call x4, Pallas kernels, comm_call(): pl.pallas_call(kernel, out_shape=out_shape, in_specs=in_specs, out_specs=...  210 us
    pallas_call x2, Pallas kernels, expert_backward(): pl.pallas_call(functools.partial(bwd_kernel, layer, capacity, groups, len...  130 us
    pallas_call x1, Pallas kernels, expert_forward(): pl.pallas_call(functools.partial(fwd_kernel, layer, capacity, groups), ou...  63 us
    ppermute x9, waiting for transfers between devices, send_over(): return lax.ppermute(x, 'ep', [(i, i ^ flip) for i in range(4)])  18.9 us
    pallas_call x1, Pallas kernels, place(): pl.pallas_call(place_kernel, out_shape=(shape, shape, shape), grid_spec=p...  13.3 us
    ppermute x9, starting transfers between devices, send_over(): return lax.ppermute(x, 'ep', [(i, i ^ flip) for i in range(4)])  9.79 us
  transfers between devices with their start and end apart: 15, of which 3 were waited for; matrix products, arithmetic and copies ran while one was open for 0% of the time, Pallas kernels for 34%

profile of v4, /device:TPU:0, one launch (start us, length us, event | category | flops | bytes accessed | tf_op | source)
XLA Modules:
  0.0 458.6 jit_solution(16928014159387672272)
XLA Ops:
  0.6 0.8 convert_bitcast_fusion
  1.4 1.4 pad_maximum_fusion.4
  2.9 37.0 %shard_map.170 = (bf16[8,448,768]{2,1,0:T(8,128)(2,1)}, f32[8,32,768]{2,1,0:T(8,128)}, bf16[448,768]{1,0:T(8,128)(2,1)}) custom-call(bf16[448,768]{1,0:T(8,128)(2,1)} %bitcast.42, bf16[2,448,448]{2,1,0:T(8,128)(2,1)} %w_dense_ref.7, f32[32,768]{1,0:T(8,128)} %bitcast.46), custom_call_target="tpu_custom_call" | custom-call | flops 20000000000 | bytes 20000000 | tf_op jit(solution)/shard_map/pallas_call | solution.py:644
  39.9 0.1 collective-permute-start.3
  40.0 1.5 collective-permute-start.2
  41.5 1.0 collective-permute-start.1
  42.5 1.1 collective-permute-start
  43.5 0.6 pad_add_fusion.base_ref
  44.1 63.0 %shard_map.171 = (f32[8,448,768]{2,1,0:T(8,128)}, bf16[6,8,256,480]{3,2,1,0:T(8,128)(2,1)}) custom-call(s32[3]{0:T(128)} %pad_add_fusion.base_ref, f32[8,32,768]{2,1,0:T(8,128)} %get-tuple-element.44.meta_ref, bf16[2,96,448,128]{3,2,1,0:T(8,128)(2,1)} %w1_ref.5, bf16[2,96,448,128]{3,2,1,0:T(8,128)(2,1)} %w3_ref.5, bf16[2,96,448,128]{3,2,1,0:T(8,128)(2,1)} %bitcast.32, ...), custom_call_target="tpu_custom_call" | custom-call | flops 20000000000 | bytes 20000000 | tf_op jit(solution)/shard_map/pallas_call | solution.py:358
  107.1 0.0 collective-permute-done.2.refs_4_
  107.1 0.0 collective-permute-start.6
  107.1 0.0 collective-permute-done.1.refs_3_
  107.1 0.5 collective-permute-start.5
  107.6 0.0 collective-permute-done.refs_2_
  107.6 0.0 collective-permute-start.4
  107.7 80.1 %shard_map.172 = (bf16[8,448,768]{2,1,0:T(8,128)(2,1)}, bf16[448,768]{1,0:T(8,128)(2,1)}, bf16[448,768]{1,0:T(8,128)(2,1)}) custom-call(f32[8,448,768]{2,1,0:T(8,128)} %get-tuple-element.48.part_ref, bf16[448,768]{1,0:T(8,128)(2,1)} %get-tuple-element.49.u1_ref, bf16[2,448,128]{2,1,0:T(8,128)(2,1)} %ws_gate_ref.3, bf16[2,448,128]{2,1,0:T(8,128)(2,1)} %ws_up_ref.3, ...), custom_call_target="tpu_custom_call" | custom-call | flops 20000000000 | bytes 20000000 | tf_op jit(solution)/shard_map/pallas_call | solution.py:644
  187.7 0.0 collective-permute-done.3.refs_5_
  187.8 0.0 copy-start.2
  187.8 0.0 collective-permute-done.6.refs_8_
  187.8 0.0 collective-permute-done.5.refs_7_
  187.8 0.0 collective-permute-done.4.refs_6_
  187.8 0.8 copy-done.2
  188.6 67.6 %shard_map.173 = (bf16[8,448,768]{2,1,0:T(8,128)(2,1)}, bf16[2,96,448,128]{3,2,1,0:T(8,128)(2,1)}, bf16[2,96,448,128]{3,2,1,0:T(8,128)(2,1)}, bf16[2,96,448,128]{3,2,1,0:T(8,128)(2,1)}) custom-call(s32[3]{0:T(128)} %pad_add_fusion.base_ref, f32[8,32,768]{2,1,0:T(8,128)} %get-tuple-element.44.meta_ref, bf16[2,96,448,128]{3,2,1,0:T(8,128)(2,1)} %w1_ref.5, ...), custom_call_target="tpu_custom_call" | custom-call | flops 20000000000 | bytes 20000000 | tf_op jit(solution)/shard_map/pallas_call | solution.py:395
  256.2 58.5 %shard_map.174 = (bf16[8,448,768]{2,1,0:T(8,128)(2,1)}, bf16[3,48,448,128]{3,2,1,0:T(8,128)(2,1)}, bf16[448,768]{1,0:T(8,128)(2,1)}, f32[448,768]{1,0:T(8,128)}, bf16[224,1280]{1,0:T(8,128)(2,1)}) custom-call(bf16[8,448,768]{2,1,0:T(8,128)(2,1)} %get-tuple-element.52.part_ref, bf16[2,96,448,128]{3,2,1,0:T(8,128)(2,1)} %get-tuple-element.53.d1_ref.refs_3_, ...), custom_call_target="tpu_custom_call" | custom-call | flops 20000000000 | bytes 20000000 | tf_op jit(solution)/shard_map/pallas_call | solution.py:644
  314.7 62.6 %shard_map.175 = (bf16[8,448,768]{2,1,0:T(8,128)(2,1)}, bf16[2,96,448,128]{3,2,1,0:T(8,128)(2,1)}, bf16[2,96,448,128]{3,2,1,0:T(8,128)(2,1)}, bf16[2,96,448,128]{3,2,1,0:T(8,128)(2,1)}) custom-call(s32[3]{0:T(128)} %pad_add_fusion.base_ref, f32[8,32,768]{2,1,0:T(8,128)} %get-tuple-element.44.meta_ref, ...), custom_call_target="tpu_custom_call", output_to_operand_aliasing={{1}: (8, {}), {2}: (9, {}), {3}: (10, {})} | custom-call | flops 20000000000 | bytes 20000000 | tf_op jit(solution)/shard_map/pallas_call | solution.py:395
  377.4 34.5 %shard_map.176 = (bf16[448,768]{1,0:T(8,128)(2,1)}, bf16[3,48,448,128]{3,2,1,0:T(8,128)(2,1)}, bf16[224,448]{1,0:T(8,128)(2,1)}) custom-call(bf16[8,448,768]{2,1,0:T(8,128)(2,1)} %get-tuple-element.62.part_ref, bf16[2,96,448,128]{3,2,1,0:T(8,128)(2,1)} %get-tuple-element.63.d1_ref.refs_0_, bf16[2,96,448,128]{3,2,1,0:T(8,128)(2,1)} %get-tuple-element.64.d3_ref.refs_1_, ...), custom_call_target="tpu_custom_call" | custom-call | flops 20000000000 | bytes 20000000 | tf_op jit(solution)/shard_map/pallas_call | solution.py:644
  411.9 1.5 collective-permute-start.9
  413.4 1.5 collective-permute-start.13
  414.8 0.7 collective-permute-start.12
  415.5 1.4 collective-permute-start.11
  416.9 0.7 collective-permute-start.8
  417.5 4.1 collective-permute-done.9
  421.6 0.7 collective-permute-start.7
  422.3 0.0 copy-done.5
  422.3 13.3 %shard_map.177 = (bf16[2,96,448,128]{3,2,1,0:T(8,128)(2,1)}, bf16[2,96,448,128]{3,2,1,0:T(8,128)(2,1)}, bf16[2,96,448,128]{3,2,1,0:T(8,128)(2,1)}) custom-call(s32[3]{0:T(128)} %pad_add_fusion.base_ref, bf16[3,48,448,128]{3,2,1,0:T(8,128)(2,1)} %get-tuple-element.69.recv_ref, ...), custom_call_target="tpu_custom_call", output_to_operand_aliasing={{0}: (2, {}), {1}: (3, {}), {2}: (4, {})} | custom-call | flops 20000000000 | bytes 20000000 | tf_op jit(solution)/shard_map/pallas_call | solution.py:435
  435.6 14.9 %collective-permute-done.8 = bf16[224,448]{1,0:T(8,128)(2,1)} collective-permute-done((bf16[224,448]{1,0:T(8,128)(2,1)}, bf16[224,448]{1,0:T(8,128)(2,1)}, u32[]{:S(2)}, u32[]{:S(2)}) %collective-permute-start.8) | collective-permute-done | bytes 200736 | tf_op jit(solution)/shard_map/ppermute | solution.py:785
  450.5 0.0 collective-permute-done.11
  450.5 1.3 add_convert_fusion
  451.9 0.0 collective-permute-start.14
  451.9 1.3 add_convert_fusion.1
  453.2 0.5 collective-permute-start.10
  453.7 1.1 collective-permute-done.10
  454.9 0.1 broadcast_select_fusion
  455.1 0.1 fusion.12
  455.2 0.7 maximum_bitcast_fusion.1
  455.9 1.0 pad_maximum_fusion
  456.9 0.8 pad_maximum_fusion.1
  457.7 0.8 copy.32
  (16 shorter events, 0.1 us)
Async XLA Ops:
  2.9 37.0 %copy-start = (bf16[768,448]{0,1:T(8,128)(2,1)S(1)}, bf16[768,448]{0,1:T(8,128)(2,1)}, u32[]{:S(2)}) copy-start(bf16[768,448]{0,1:T(8,128)(2,1)} %param.12) | copy-start | bytes 2064388
  39.9 147.8 %collective-permute-start.3 = (bf16[448,768]{1,0:T(8,128)(2,1)S(1)}, bf16[448,768]{1,0:T(8,128)(2,1)S(1)}, u32[]{:S(2)}, u32[]{:S(2)}) collective-permute-start(bf16[448,768]{1,0:T(8,128)(2,1)S(1)} %bitcast.37), channel_id=1, source_target_pairs={{0,1},{1,0},{2,3},{3,2},{4,5},{5,4},{6,7},{7,6}} | collective-permute-start | bytes 2064392 | tf_op jit(solution)/shard_map/ppermute | solution.py:789
  40.0 67.0 %collective-permute-start.2 = (bf16[448,768]{1,0:T(8,128)(2,1)S(1)}, bf16[448,768]{1,0:T(8,128)(2,1)}, u32[]{:S(2)}, u32[]{:S(2)}) collective-permute-start(bf16[448,768]{1,0:T(8,128)(2,1)S(1)} %bitcast.38), channel_id=1, source_target_pairs={{0,6},{2,4},{4,2},{6,0},{1,7},{3,5},{5,3},{7,1}} | collective-permute-start | bytes 2064392 | tf_op jit(solution)/shard_map/ppermute | solution.py:785
  41.5 65.6 %collective-permute-start.1 = (bf16[448,768]{1,0:T(8,128)(2,1)S(1)}, bf16[448,768]{1,0:T(8,128)(2,1)}, u32[]{:S(2)}, u32[]{:S(2)}) collective-permute-start(bf16[448,768]{1,0:T(8,128)(2,1)S(1)} %bitcast.39), channel_id=1, source_target_pairs={{0,4},{2,6},{4,0},{6,2},{1,5},{3,7},{5,1},{7,3}} | collective-permute-start | bytes 2064392 | tf_op jit(solution)/shard_map/ppermute | solution.py:785
  42.5 65.2 %collective-permute-start = (bf16[448,768]{1,0:T(8,128)(2,1)S(1)}, bf16[448,768]{1,0:T(8,128)(2,1)}, u32[]{:S(2)}, u32[]{:S(2)}) collective-permute-start(bf16[448,768]{1,0:T(8,128)(2,1)S(1)} %bitcast.40), channel_id=1, source_target_pairs={{0,2},{2,0},{4,6},{6,4},{1,3},{3,1},{5,7},{7,5}} | collective-permute-start | bytes 2064392 | tf_op jit(solution)/shard_map/ppermute | solution.py:785
  107.1 80.7 %collective-permute-start.6 = (bf16[448,768]{1,0:T(8,128)(2,1)}, bf16[448,768]{1,0:T(8,128)(2,1)}, u32[]{:S(2)}, u32[]{:S(2)}) collective-permute-start(bf16[448,768]{1,0:T(8,128)(2,1)} %collective-permute-done.2.refs_4_), channel_id=1, source_target_pairs={{0,1},{1,0},{2,3},{3,2},{4,5},{5,4},{6,7},{7,6}} | collective-permute-start | bytes 2064392 | tf_op jit(solution)/shard_map/ppermute | solution.py:789
  107.1 80.6 %collective-permute-start.5 = (bf16[448,768]{1,0:T(8,128)(2,1)}, bf16[448,768]{1,0:T(8,128)(2,1)}, u32[]{:S(2)}, u32[]{:S(2)}) collective-permute-start(bf16[448,768]{1,0:T(8,128)(2,1)} %collective-permute-done.1.refs_3_), channel_id=1, source_target_pairs={{0,1},{1,0},{2,3},{3,2},{4,5},{5,4},{6,7},{7,6}} | collective-permute-start | bytes 2064392 | tf_op jit(solution)/shard_map/ppermute | solution.py:789
  107.6 80.2 %collective-permute-start.4 = (bf16[448,768]{1,0:T(8,128)(2,1)}, bf16[448,768]{1,0:T(8,128)(2,1)}, u32[]{:S(2)}, u32[]{:S(2)}) collective-permute-start(bf16[448,768]{1,0:T(8,128)(2,1)} %collective-permute-done.refs_2_), channel_id=1, source_target_pairs={{0,1},{1,0},{2,3},{3,2},{4,5},{5,4},{6,7},{7,6}} | collective-permute-start | bytes 2064392 | tf_op jit(solution)/shard_map/ppermute | solution.py:789
  187.8 0.8 copy-start.2
  377.4 36.0 %copy-start.3 = (bf16[224,1280]{1,0:T(8,128)(2,1)S(1)}, bf16[224,1280]{1,0:T(8,128)(2,1)}, u32[]{:S(2)}) copy-start(bf16[224,1280]{1,0:T(8,128)(2,1)} %get-tuple-element.76) | copy-start | bytes 1720324
  411.9 9.7 %collective-permute-start.9 = (bf16[224,448]{1,0:T(8,128)(2,1)}, bf16[224,448]{1,0:T(8,128)(2,1)S(1)}, u32[]{:S(2)}, u32[]{:S(2)}) collective-permute-start(bf16[224,448]{1,0:T(8,128)(2,1)} %get-tuple-element.72), channel_id=1, source_target_pairs={{0,6},{2,4},{4,2},{6,0},{1,7},{3,5},{5,3},{7,1}} | collective-permute-start | bytes 602120 | tf_op jit(solution)/shard_map/ppermute | solution.py:785
  413.4 37.1 %collective-permute-start.13 = (bf16[224,1280]{1,0:T(8,128)(2,1)S(1)}, bf16[224,1280]{1,0:T(8,128)(2,1)S(1)}, u32[]{:S(2)}, u32[]{:S(2)}) collective-permute-start(bf16[224,1280]{1,0:T(8,128)(2,1)S(1)} %copy-done.3), channel_id=1, source_target_pairs={{0,6},{2,4},{4,2},{6,0},{1,7},{3,5},{5,3},{7,1}} | collective-permute-start | bytes 1720328 | tf_op jit(solution)/shard_map/ppermute | solution.py:785
  414.8 35.7 %collective-permute-start.12 = (bf16[224,1280]{1,0:T(8,128)(2,1)S(1)}, bf16[224,1280]{1,0:T(8,128)(2,1)S(1)}, u32[]{:S(2)}, u32[]{:S(2)}) collective-permute-start(bf16[224,1280]{1,0:T(8,128)(2,1)S(1)} %copy-done.3), channel_id=1, source_target_pairs={{0,4},{2,6},{4,0},{6,2},{1,5},{3,7},{5,1},{7,3}} | collective-permute-start | bytes 1720328 | tf_op jit(solution)/shard_map/ppermute | solution.py:785
  415.5 35.0 %collective-permute-start.11 = (bf16[224,1280]{1,0:T(8,128)(2,1)S(1)}, bf16[224,1280]{1,0:T(8,128)(2,1)}, u32[]{:S(2)}, u32[]{:S(2)}) collective-permute-start(bf16[224,1280]{1,0:T(8,128)(2,1)S(1)} %copy-done.3), channel_id=1, source_target_pairs={{0,2},{2,0},{4,6},{6,4},{1,3},{3,1},{5,7},{7,5}} | collective-permute-start | bytes 1720328 | tf_op jit(solution)/shard_map/ppermute | solution.py:785
  416.9 33.6 %collective-permute-start.8 = (bf16[224,448]{1,0:T(8,128)(2,1)}, bf16[224,448]{1,0:T(8,128)(2,1)}, u32[]{:S(2)}, u32[]{:S(2)}) collective-permute-start(bf16[224,448]{1,0:T(8,128)(2,1)} %get-tuple-element.72), channel_id=1, source_target_pairs={{0,4},{2,6},{4,0},{6,2},{1,5},{3,7},{5,1},{7,3}} | collective-permute-start | bytes 602120 | tf_op jit(solution)/shard_map/ppermute | solution.py:785
  421.6 0.7 copy-start.5
  421.6 28.9 %collective-permute-start.7 = (bf16[224,448]{1,0:T(8,128)(2,1)}, bf16[224,448]{1,0:T(8,128)(2,1)}, u32[]{:S(2)}, u32[]{:S(2)}) collective-permute-start(bf16[224,448]{1,0:T(8,128)(2,1)} %get-tuple-element.72), channel_id=1, source_target_pairs={{0,2},{2,0},{4,6},{6,4},{1,3},{3,1},{5,7},{7,5}} | collective-permute-start | bytes 602120 | tf_op jit(solution)/shard_map/ppermute | solution.py:785
  422.3 29.6 %copy-start.4 = (bf16[224,448]{1,0:T(8,128)(2,1)S(1)}, bf16[224,448]{1,0:T(8,128)(2,1)}, u32[]{:S(2)}) copy-start(bf16[224,448]{1,0:T(8,128)(2,1)} %get-tuple-element.72) | copy-start | bytes 602116
  451.9 3.1 collective-permute-start.14
  453.2 4.5 copy-start.1
  453.2 1.6 collective-permute-start.10
